TPU v7x, 16 devices: a whole 2x2x2 slice. The times are simulated.
16 devices in a mesh: data: 2 (over z), stage: 8 (over y, x, core).
Axes of the slice: x: 2, y: 2, z: 2, core: 2. Of those that a mesh axis runs over, the one named last changes fastest.
Arguments:
- x_enc: bfloat16 [16, 1536, 1536], P(('data', 'stage'))
- h_dec: bfloat16 [16, 64, 1536], P(('data', 'stage'))
- cot_out: bfloat16 [16, 64, 1536], P(('data', 'stage'))
- enc_up: bfloat16 [1, 1536, 8960], replicated
- enc_down: bfloat16 [1, 8960, 1536], replicated
- w_key: bfloat16 [1, 1536, 2, 128], replicated
- w_val: bfloat16 [1, 1536, 2, 128], replicated
- w_query: bfloat16 [1, 1536, 1536], replicated
- w_out: bfloat16 [1, 1536, 1536], replicated
- w_ff1: bfloat16 [1, 1536, 8960], replicated
- w_ff2: bfloat16 [1, 8960, 1536], replicated
Outputs:
- output 1: bfloat16 [16, 1536, 1536], P(('data', 'stage'))
- output 2: bfloat16 [16, 64, 1536], P(('data', 'stage'))
- output 3: float32 [1, 1536, 8960], P(None, ('data', 'stage'))
- output 4: float32 [1, 8960, 1536], P(None, ('data', 'stage'))
- output 5: float32 [1, 1536, 2, 128], P(None, ('data', 'stage'))
- output 6: float32 [1, 1536, 2, 128], P(None, ('data', 'stage'))
- output 7: float32 [1, 1536, 1536], P(None, ('data', 'stage'))
- output 8: float32 [1, 1536, 1536], P(None, ('data', 'stage'))
- output 9: float32 [1, 1536, 8960], P(None, ('data', 'stage'))
- output 10: float32 [1, 8960, 1536], P(None, ('data', 'stage'))
All inputs are finite; a program needn't handle non-finite values.
Results may differ from a plain program's by a relative error of at most 0.02.
Values are sent between devices in bfloat16 or wider.
A program may use at most 1 GiB of HBM per device.

v0:
```python
import jax
import jax.numpy as jnp
from jax import lax
from jax.sharding import PartitionSpec as P


def mlp_forward(hidden, w_a, w_b):
    pre_act = jnp.einsum('bsd,df->bsf', hidden, w_a, preferred_element_type=jnp.float32)
    hidden_act = jax.nn.gelu(pre_act).astype(jnp.bfloat16)
    out_sum = hidden.astype(jnp.float32) + jnp.einsum('bsf,fd->bsd', hidden_act, w_b, preferred_element_type=jnp.float32)
    return out_sum.astype(jnp.bfloat16)


def mlp_backward(hidden, w_a, w_b, grad_out):
    pre_act = jnp.einsum('bsd,df->bsf', hidden, w_a, preferred_element_type=jnp.float32)
    hidden_act, gelu_pull = jax.vjp(jax.nn.gelu, pre_act)
    grad_act = jnp.einsum('bsd,fd->bsf', grad_out, w_b, preferred_element_type=jnp.float32).astype(jnp.bfloat16)
    grad_pre = gelu_pull(grad_act.astype(jnp.float32))[0].astype(jnp.bfloat16)
    grad_in = (grad_out.astype(jnp.float32) + jnp.einsum('bsf,df->bsd', grad_pre, w_a, preferred_element_type=jnp.float32)).astype(jnp.bfloat16)
    grad_wa = jnp.einsum('bsd,bsf->df', hidden, grad_pre, preferred_element_type=jnp.float32)
    grad_wb = jnp.einsum('bsf,bsd->fd', hidden_act.astype(jnp.bfloat16), grad_out, preferred_element_type=jnp.float32)
    return grad_in, grad_wa, grad_wb


def split_heads(proj, k_mem):
    batch, seq_len, width = proj.shape
    kv_heads, head_dim = k_mem.shape[-2], k_mem.shape[-1]
    return proj.reshape(batch, seq_len, kv_heads, width // (kv_heads * head_dim), head_dim)


def attn_probs(query, k_mem):
    logits = jnp.einsum('bqkgh,bskh->bkgqs', query, k_mem, preferred_element_type=jnp.float32)
    return jax.nn.softmax(logits * k_mem.shape[-1] ** -0.5, axis=-1)


def attn_forward(hidden, k_mem, v_mem, w_q, w_o):
    query = split_heads(jnp.einsum('bsd,de->bse', hidden, w_q, preferred_element_type=jnp.float32).astype(jnp.bfloat16), k_mem)
    attn_prob = attn_probs(query, k_mem).astype(jnp.bfloat16)
    context = jnp.einsum('bkgqs,bskh->bqkgh', attn_prob, v_mem, preferred_element_type=jnp.float32).astype(jnp.bfloat16)
    out_sum = hidden.astype(jnp.float32) + jnp.einsum('bse,ed->bsd', context.reshape(hidden.shape), w_o, preferred_element_type=jnp.float32)
    return out_sum.astype(jnp.bfloat16)


def attn_backward(hidden, k_mem, v_mem, w_q, w_o, grad_out):
    query = split_heads(jnp.einsum('bsd,de->bse', hidden, w_q, preferred_element_type=jnp.float32).astype(jnp.bfloat16), k_mem)
    attn_prob = attn_probs(query, k_mem)
    prob_bf = attn_prob.astype(jnp.bfloat16)
    context = jnp.einsum('bkgqs,bskh->bqkgh', prob_bf, v_mem, preferred_element_type=jnp.float32).astype(jnp.bfloat16)
    grad_wo = jnp.einsum('bse,bsd->ed', context.reshape(hidden.shape), grad_out, preferred_element_type=jnp.float32)
    grad_ctx = split_heads(jnp.einsum('bsd,ed->bse', grad_out, w_o, preferred_element_type=jnp.float32).astype(jnp.bfloat16), k_mem)
    grad_prob = jnp.einsum('bqkgh,bskh->bkgqs', grad_ctx, v_mem, preferred_element_type=jnp.float32)
    grad_v = jnp.einsum('bkgqs,bqkgh->bskh', prob_bf, grad_ctx, preferred_element_type=jnp.float32).astype(jnp.bfloat16)
    scale_val = k_mem.shape[-1] ** -0.5
    grad_logit = (attn_prob * (grad_prob - jnp.sum(attn_prob * grad_prob, axis=-1, keepdims=True)) * scale_val).astype(jnp.bfloat16)
    grad_query = jnp.einsum('bkgqs,bskh->bqkgh', grad_logit, k_mem, preferred_element_type=jnp.float32).astype(jnp.bfloat16).reshape(hidden.shape)
    grad_k = jnp.einsum('bkgqs,bqkgh->bskh', grad_logit, query, preferred_element_type=jnp.float32).astype(jnp.bfloat16)
    grad_wq = jnp.einsum('bsd,bse->de', hidden, grad_query, preferred_element_type=jnp.float32)
    grad_in = (grad_out.astype(jnp.float32) + jnp.einsum('bse,de->bsd', grad_query, w_q, preferred_element_type=jnp.float32)).astype(jnp.bfloat16)
    return grad_in, grad_k, grad_v, grad_wq, grad_wo


def solution(mesh):
    stage_size = mesh.shape['stage']
    partner_perm = [(index, (index + stage_size // 2) % stage_size) for index in range(stage_size)]
    row_spec = P(('data', 'stage'), None, None)
    full_spec3 = P(None, None, None)
    full_spec4 = P(None, None, None, None)
    grad_spec3 = P(None, ('data', 'stage'), None)
    grad_spec4 = P(None, ('data', 'stage'), None, None)

    def scatter_grad(stacked):
        return lax.psum_scatter(stacked, ('data', 'stage'), scatter_dimension=1, tiled=True)

    def body(x_enc, h_dec, cot_out, enc_up, enc_down, w_key, w_val, w_query, w_out, w_ff1, w_ff2):
        enc_saved = []
        memory = x_enc
        for layer in range(enc_up.shape[0]):
            enc_saved.append(memory)
            memory = mlp_forward(memory, enc_up[layer], enc_down[layer])
        key_all = jnp.einsum('bsd,ldkh->lbskh', memory, w_key, preferred_element_type=jnp.float32).astype(jnp.bfloat16)
        val_all = jnp.einsum('bsd,ldkh->lbskh', memory, w_val, preferred_element_type=jnp.float32).astype(jnp.bfloat16)
        key_recv = lax.ppermute(key_all, 'stage', partner_perm)
        val_recv = lax.ppermute(val_all, 'stage', partner_perm)
        dec_in = []
        dec_mid = []
        hidden = h_dec
        for layer in range(w_key.shape[0]):
            dec_in.append(hidden)
            mid_out = attn_forward(hidden, key_recv[layer], val_recv[layer], w_query[layer], w_out[layer])
            dec_mid.append(mid_out)
            hidden = mlp_forward(mid_out, w_ff1[layer], w_ff2[layer])
        grad_h = cot_out
        key_grads = []
        val_grads = []
        query_grads = []
        out_grads = []
        ff1_grads = []
        ff2_grads = []
        for layer in reversed(range(w_key.shape[0])):
            grad_h, grad_a, grad_b = mlp_backward(dec_mid[layer], w_ff1[layer], w_ff2[layer], grad_h)
            grad_h, grad_k, grad_v, grad_wq, grad_wo = attn_backward(dec_in[layer], key_recv[layer], val_recv[layer], w_query[layer], w_out[layer], grad_h)
            key_grads.append(grad_k)
            val_grads.append(grad_v)
            query_grads.append(grad_wq)
            out_grads.append(grad_wo)
            ff1_grads.append(grad_a)
            ff2_grads.append(grad_b)
        key_back = lax.ppermute(jnp.stack(key_grads[::-1]), 'stage', partner_perm)
        val_back = lax.ppermute(jnp.stack(val_grads[::-1]), 'stage', partner_perm)
        grad_key = jnp.einsum('bsd,lbskh->ldkh', memory, key_back, preferred_element_type=jnp.float32)
        grad_val = jnp.einsum('bsd,lbskh->ldkh', memory, val_back, preferred_element_type=jnp.float32)
        grad_mem = (jnp.einsum('lbskh,ldkh->bsd', key_back, w_key, preferred_element_type=jnp.float32)
                    + jnp.einsum('lbskh,ldkh->bsd', val_back, w_val, preferred_element_type=jnp.float32)).astype(jnp.bfloat16)
        up_grads = []
        down_grads = []
        for layer in reversed(range(enc_up.shape[0])):
            grad_mem, grad_a, grad_b = mlp_backward(enc_saved[layer], enc_up[layer], enc_down[layer], grad_mem)
            up_grads.append(grad_a)
            down_grads.append(grad_b)
        return (grad_mem, grad_h,
                scatter_grad(jnp.stack(up_grads[::-1])), scatter_grad(jnp.stack(down_grads[::-1])),
                scatter_grad(grad_key), scatter_grad(grad_val),
                scatter_grad(jnp.stack(query_grads[::-1])), scatter_grad(jnp.stack(out_grads[::-1])),
                scatter_grad(jnp.stack(ff1_grads[::-1])), scatter_grad(jnp.stack(ff2_grads[::-1])))

    return jax.shard_map(body, mesh=mesh,
                         in_specs=(row_spec, row_spec, row_spec, full_spec3, full_spec3, full_spec4, full_spec4, full_spec3, full_spec3, full_spec3, full_spec3),
                         out_specs=(row_spec, row_spec, grad_spec3, grad_spec3, grad_spec4, grad_spec4, grad_spec3, grad_spec3, grad_spec3, grad_spec3),
                         check_vma=False)
```

profile of v0, /device:TPU:0, one launch (start us, length us, event | category | flops | bytes accessed | tf_op | source)
XLA Modules:
  0.0 1908.3 jit_solution(3851584180794900344)
XLA Ops:
  7.2 50.9 %fusion.21 = f32[1536,8960]{1,0:T(8,128)} fusion(bf16[1,1536,8960]{2,1,0:T(8,128)(2,1)} %param.14, bf16[1,1536,1536]{2,1,0:T(8,128)(2,1)} %param.11), kind=kOutput, calls=%fused_computation.31 | convolution fusion | flops 42278584320 | bytes 87293952 | tf_op jit(solution)/shard_map/bsd,df->bsf/dot_general | solution.py:8
  58.1 59.4 %fusion.38 = bf16[1536,1536,1]{1,0,2:T(8,128)(2,1)} fusion(bf16[1,8960,1536]{2,1,0:T(8,128)(2,1)} %param.15, bf16[1,1536,1536]{2,1,0:T(8,128)(2,1)} %param.11, f32[1536,8960]{1,0:T(8,128)} %fusion.21), kind=kOutput, calls=%fused_computation.43 | convolution fusion | flops 42409525248 | bytes 92012544 | tf_op jit(solution)/shard_map/bsf,fd->bsd/dot_general | solution.py:10
  117.6 4.8 fusion.60
  129.1 14.9 collective-permute-done
  145.8 14.2 collective-permute-done.1
  166.2 11.4 fusion.12
  177.6 15.2 fusion.108
  192.8 13.9 fusion.87
  223.7 5.1 convolution_bitcast_fusion.5
  228.8 23.3 %copy.66 = f32[1,1536,1536]{2,0,1:T(1,128)} copy(f32[1,1536,1536]{1,2,0:T(8,128)} %convolution_bitcast_fusion.5) | data formatting | bytes 18874368 | tf_op jit(solution)/shard_map/stack | solution.py:123
  265.9 4.9 fusion.29
  270.8 80.8 %fusion.2 = bf16[1536,8960]{1,0:T(8,128)(2,1)} fusion(f32[1536,8960]{1,0:T(8,128)} %fusion.21, bf16[1536,1536]{1,0:T(8,128)(2,1)} %fusion.29, bf16[1,8960,1536]{2,1,0:T(8,128)(2,1)} %param.15), kind=kOutput, calls=%fused_computation.6 | convolution fusion | flops 42581360640 | bytes 114819072 | tf_op jit(solution)/shard_map/bsd,fd->bsf/dot_general | solution.py:17
  351.7 51.4 %convolution_bitcast_fusion.2 = f32[1,1536,8960]{1,2,0:T(8,128)} fusion(bf16[1536,8960]{1,0:T(8,128)(2,1)} %fusion.2, bf16[1,1536,1536]{2,1,0:T(8,128)(2,1)} %param.11), kind=kOutput, calls=%fused_computation.17 | convolution fusion | flops 42278584320 | bytes 87293952 | tf_op jit(solution)/shard_map/bsd,bsf->df/dot_general | solution.py:20
  403.1 110.2 %copy.63 = f32[1,1536,8960]{2,0,1:T(1,128)} copy(f32[1,1536,8960]{1,2,0:T(8,128)} %convolution_bitcast_fusion.2) | data formatting | bytes 110100480 | tf_op jit(solution)/shard_map/stack | solution.py:121
  514.3 5.0 convolution_bitcast_fusion.4
  520.9 21.2 %convolution_bitcast_fusion.3 = f32[1,8960,1536]{2,1,0:T(8,128)} fusion(f32[64,8960]{1,0:T(8,128)S(1)} %copy-done.4, bf16[1,64,1536]{2,1,0:T(8,128)(2,1)S(1)} %copy-done.16), kind=kOutput, calls=%fused_computation.18 | convolution fusion | flops 1766768640 | bytes 57540608 | tf_op jit(solution)/shard_map/bsf,bsd->fd/dot_general | solution.py:21
  543.3 21.3 %convolution_bitcast_fusion = f32[1,1536,8960]{2,1,0:T(8,128)} fusion(bf16[64,1536]{1,0:T(8,128)(2,1)S(1)} %copy-done.18, bf16[64,8960]{1,0:T(8,128)(2,1)S(1)} %copy-done.5), kind=kOutput, calls=%fused_computation.15 | convolution fusion | flops 1761607680 | bytes 56393728 | tf_op jit(solution)/shard_map/bsd,bsf->df/dot_general | solution.py:20
  564.8 59.3 %convolution_bitcast_fusion.1 = f32[1,8960,1536]{2,1,0:T(8,128)} fusion(bf16[1536,1536]{1,0:T(8,128)(2,1)} %fusion.29, f32[1536,8960]{1,0:T(8,128)} %fusion.21), kind=kOutput, calls=%fused_computation.16 | convolution fusion | flops 42402447360 | bytes 114819072 | tf_op jit(solution)/shard_map/bsf,bsd->fd/dot_general | solution.py:21
  629.6 57.3 %fusion.35 = bf16[1,1536,1536]{2,1,0:T(8,128)(2,1)} fusion(bf16[1536,8960]{1,0:T(8,128)(2,1)} %fusion.2, bf16[1,1536,8960]{2,1,0:T(8,128)(2,1)} %param.14, bf16[1536,1536]{1,0:T(8,128)(2,1)} %fusion.29), kind=kOutput, calls=%fused_computation.42 | convolution fusion | flops 42285662208 | bytes 64487424 | tf_op jit(solution)/shard_map/bsf,df->bsd/dot_general | solution.py:19
  690.5 311.3 %all-reduce.8.cloned.1.call-done = f32[1,1536,8960]{2,0,1:T(1,128)} async-done(((f32[1,1536,8960]{2,0,1:T(1,128)}), f32[1,1536,8960]{2,0,1:T(1,128)}) %all-reduce.8.cloned.1.call-update) | async-done | bytes 55050256
  1006.1 80.5 %reduce-scatter.7.cloned.1.call-done = f32[1,96,1536]{2,1,0:T(8,128)} async-done(((f32[1,1536,1536]{2,1,0:T(8,128)}), f32[1,96,1536]{2,1,0:T(8,128)}) %reduce-scatter.7.cloned.1.call-update) | async-done | bytes 589840 | tf_op jit(solution)/shard_map/reduce_scatter | solution.py:72
  1086.7 271.5 %reduce-scatter.11.cloned.1.call-done = f32[1,560,1536]{2,1,0:T(8,128)} async-done(((f32[1,8960,1536]{2,1,0:T(8,128)}), f32[1,560,1536]{2,1,0:T(8,128)}) %reduce-scatter.11.cloned.1.call-update) | async-done | bytes 3440656 | tf_op jit(solution)/shard_map/reduce_scatter | solution.py:72
  1358.1 271.4 %reduce-scatter.9.cloned.1.call-done = f32[1,96,8960]{2,1,0:T(8,128)} async-done(((f32[1,1536,8960]{2,1,0:T(8,128)}), f32[1,96,8960]{2,1,0:T(8,128)}) %reduce-scatter.9.cloned.1.call-update) | async-done | bytes 3440656 | tf_op jit(solution)/shard_map/reduce_scatter | solution.py:72
  1629.6 271.5 %reduce-scatter.5.cloned.1.call-done = f32[1,560,1536]{2,1,0:T(8,128)} async-done(((f32[1,8960,1536]{2,1,0:T(8,128)}), f32[1,560,1536]{2,1,0:T(8,128)}) %reduce-scatter.5.cloned.1.call-update) | async-done | bytes 3440656 | tf_op jit(solution)/shard_map/reduce_scatter | solution.py:72
  (110 shorter events, 62.8 us)
Async XLA Ops:
  7.2 110.4 %copy-start = (bf16[1,1536,2,128]{3,2,1,0:T(2,128)(2,1)S(1)}, bf16[1,1536,2,128]{3,2,1,0:T(2,128)(2,1)}, u32[]{:S(2)}) copy-start(bf16[1,1536,2,128]{3,2,1,0:T(2,128)(2,1)} %param.16) | copy-start | bytes 2359300
  7.2 679.7 %all-reduce.10.cloned.1.call-start = ((), (), s32[]{:S(2)}) async-start(), calls=%async_computation.9 | async-start | bytes 25165824
  117.6 8.1 copy-start.21
  117.6 8.0 copy-start.25
  117.6 10.3 slice-start.2
  122.3 5.6 slice-start.3
  122.4 21.7 %collective-permute-start = (bf16[1,1,1536,2,128]{4,2,3,1,0:T(8,128)(2,1)}, bf16[1,1,1536,2,128]{4,2,3,1,0:T(8,128)(2,1)S(1)}, u32[]{:S(2)}, u32[]{:S(2)}) collective-permute-start(bf16[1,1,1536,2,128]{4,2,3,1,0:T(8,128)(2,1)} %fusion.60), channel_id=1, source_target_pairs={{0,4},{1,5},{2,6},{3,7},{4,0},{5,1},{6,2},{7,3},{8,12},{9,13},{10,... | collective-permute-start | bytes 2359304 | tf_op jit(solution)/shard_map/ppermute | solution.py:82
  127.9 32.1 %collective-permute-start.1 = (bf16[1,1,1536,2,128]{4,2,3,1,0:T(8,128)(2,1)}, bf16[1,1,1536,2,128]{4,2,3,1,0:T(8,128)(2,1)S(1)}, u32[]{:S(2)}, u32[]{:S(2)}) collective-permute-start(bf16[1,1,1536,2,128]{4,2,3,1,0:T(8,128)(2,1)} %fusion.61), channel_id=1, source_target_pairs={{0,4},{1,5},{2,6},{3,7},{4,0},{5,1},{6,2},{7,3},{8,12},{9,13},{10,... | collective-permute-start | bytes 2359304 | tf_op jit(solution)/shard_map/ppermute | solution.py:83
  144.9 16.3 copy-start.2
  166.2 11.4 copy-start.15
  177.6 15.2 copy-start.3
  206.8 8.9 copy-start.6
  206.8 10.6 slice-start
  211.0 6.4 slice-start.1
  211.0 6.4 copy-start.24
  215.7 36.5 %collective-permute-start.3 = (bf16[1,1,1536,2,128]{2,4,3,1,0:T(8,128)(2,1)}, bf16[1,1,1536,2,128]{2,4,3,1,0:T(8,128)(2,1)}, u32[]{:S(2)}, u32[]{:S(2)}) collective-permute-start(bf16[1,1,1536,2,128]{2,4,3,1,0:T(8,128)(2,1)} %fusion.62), channel_id=1, source_target_pairs={{0,4},{1,5},{2,6},{3,7},{4,0},{5,1},{6,2},{7,3},{8,12},{9,13},{10,... | collective-permute-start | bytes 2359304 | tf_op jit(solution)/shard_map/ppermute | solution.py:109
  222.3 36.0 %collective-permute-start.2 = (bf16[1,1,1536,2,128]{2,4,3,1,0:T(8,128)(2,1)}, bf16[1,1,1536,2,128]{2,4,3,1,0:T(8,128)(2,1)S(1)}, u32[]{:S(2)}, u32[]{:S(2)}) collective-permute-start(bf16[1,1,1536,2,128]{2,4,3,1,0:T(8,128)(2,1)} %fusion.63), channel_id=1, source_target_pairs={{0,4},{1,5},{2,6},{3,7},{4,0},{5,1},{6,2},{7,3},{8,12},{9,13},{10,... | collective-permute-start | bytes 2359304 | tf_op jit(solution)/shard_map/ppermute | solution.py:108
  223.7 5.1 copy-start.11
  351.6 650.2 %all-reduce.8.cloned.1.call-start = ((), (), s32[]{:S(2)}) async-start(), calls=%async_computation.8 | async-start | bytes 110100480
  513.3 573.4 %reduce-scatter.7.cloned.1.call-start = ((), (), s32[]{:S(2)}) async-start(), calls=%async_computation.5 | async-start | bytes 10027008 | tf_op jit(solution)/shard_map/reduce_scatter | solution.py:72
  519.3 838.8 %reduce-scatter.11.cloned.1.call-start = ((), (), s32[]{:S(2)}) async-start(), calls=%async_computation.7 | async-start | bytes 58490880 | tf_op jit(solution)/shard_map/reduce_scatter | solution.py:72
  542.1 1087.5 %reduce-scatter.9.cloned.1.call-start = ((), (), s32[]{:S(2)}) async-start(), calls=%async_computation.6 | async-start | bytes 58490880 | tf_op jit(solution)/shard_map/reduce_scatter | solution.py:72
  564.7 1336.3 %reduce-scatter.5.cloned.1.call-start = ((), (), s32[]{:S(2)}) async-start(), calls=%async_computation.4 | async-start | bytes 58490880 | tf_op jit(solution)/shard_map/reduce_scatter | solution.py:72
  1001.8 899.2 %copy-start.1 = (bf16[1,1536,2,128]{3,2,1,0:T(2,128)(2,1)S(1)}, bf16[1,1536,2,128]{3,2,1,0:T(2,128)(2,1)}, u32[]{:S(2)}) copy-start(bf16[1,1536,2,128]{3,2,1,0:T(2,128)(2,1)} %param.16) | copy-start | bytes 2359300
  (16 other events, 24.1 us)
Sparse Core Ops, SparseCore 0:
  351.8 146.4 all-reduce.9
  513.4 488.3 all-reduce.7
  1007.1 79.5 reduce-scatter.6
  1092.4 265.6 reduce-scatter.10
  1363.8 265.6 reduce-scatter.8
  1635.3 265.6 reduce-scatter.4
where the time goes:
time: 1920 us; the launch traced here: 1910 us
  waiting for transfers between devices  1240 us (65%)
  matrix products  497 us (26%)
  local copies, waits for them, and re-layouts  153 us (8%)
    reduce_scatter x4, waiting for transfers between devices, scatter_grad(): lax.psum_scatter(stacked, ('data', 'stage'), scatter_dimension=1, tiled=T...  895 us
    unnamed x8, waiting for transfers between devices  311 us
    another operation x1, local copies, waits for them, and re-layouts, body(): jnp.stack(up_grads[::-1])  110 us
    dot_general x2, matrix products, mlp_backward(): jnp.einsum('bsd,fd->bsf', grad_out, w_b, preferred_element_type=jnp.float32)  96 us
    dot_general x2, matrix products, mlp_backward(): jnp.einsum('bsf,bsd->fd', hidden_act.astype(jnp.bfloat16), grad_out, pref...  80.5 us
    dot_general x2, matrix products, mlp_backward(): jnp.einsum('bsd,bsf->df', hidden, grad_pre, preferred_element_type=jnp.fl...  72.7 us
    dot_general x2, matrix products, mlp_backward(): jnp.einsum('bsf,df->bsd', grad_pre, w_a, preferred_element_type=jnp.float32)  71.2 us
    dot_general x1, matrix products, mlp_forward(): jnp.einsum('bsf,fd->bsd', hidden_act, w_b, preferred_element_type=jnp.flo...  59.4 us
  transfers between devices with their start and end apart: 10, of which 7 were waited for; matrix products, arithmetic and copies ran while one was open for 20% of the time, Pallas kernels for 0%

commit v1 on v0

v1 whole, which is shorter than its diff:
```python
import jax
import jax.numpy as jnp
from jax import lax
from jax.experimental.layout import Layout, with_layout_constraint
from jax.sharding import PartitionSpec as P


F32 = jnp.float32
BF16 = jnp.bfloat16
AXES = ('data', 'stage')


def dot(lhs, rhs, lhs_dim, rhs_dim):
    return lax.dot_general(lhs, rhs, (((lhs_dim,), (rhs_dim,)), ((), ())), preferred_element_type=F32)


def bdot(lhs, rhs, lhs_dim, rhs_dim):
    return lax.dot_general(lhs, rhs, (((lhs_dim,), (rhs_dim,)), ((0,), (0,))), preferred_element_type=F32)


def gather(rows):
    return lax.all_gather(rows, AXES, axis=0, tiled=True)


def scatter(own):
    return lax.psum_scatter(own, AXES, scatter_dimension=0, tiled=True)


def solution(mesh):
    stage_size = mesh.shape['stage']
    n_dev = mesh.shape['data'] * stage_size
    partner_perm = [(index, (index + stage_size // 2) % stage_size) for index in range(stage_size)]
    row_spec = P(AXES, None, None)
    full_spec3 = P(None, None, None)
    full_spec4 = P(None, None, None, None)
    grad_spec3 = P(None, AXES, None)
    grad_spec4 = P(None, AXES, None, None)

    def step(x_enc, h_dec, cot_out, enc_up, enc_down, w_key, w_val, w_query, w_out, w_ff1, w_ff2):
        d_model = x_enc.shape[-1]
        kv_heads, head = w_key.shape[2], w_key.shape[3]
        group = d_model // (kv_heads * head)
        kv_width = kv_heads * head
        x, up, down = x_enc[0], enc_up[0], enc_down[0]
        w_q, w_o, w_1, w_2 = w_query[0], w_out[0], w_ff1[0], w_ff2[0]
        w_kv = jnp.concatenate([w_key[0].reshape(d_model, kv_width), w_val[0].reshape(d_model, kv_width)], axis=1)

        hg = lax.ppermute(jnp.concatenate([h_dec[0], cot_out[0]], axis=1), 'stage', partner_perm)
        hid, cot = hg[:, :d_model], hg[:, d_model:]
        hg_all = gather(hg)
        hid_all, cot_all = hg_all[:, :d_model], hg_all[:, d_model:]
        s_dec = hid.shape[0]

        def heads_of(flat):
            return flat.reshape(s_dec, kv_heads, group, head).transpose(1, 2, 0, 3).reshape(kv_heads, group * s_dec, head)

        def flat_of(heads):
            return heads.reshape(kv_heads, group, s_dec, head).transpose(2, 0, 1, 3).reshape(s_dec, d_model)

        pre = dot(x, up, 1, 0)
        act, gelu_pull = jax.vjp(jax.nn.gelu, pre)
        act = act.astype(BF16)
        memory = (x.astype(F32) + dot(act, down, 1, 0)).astype(BF16)
        kv = dot(memory, w_kv, 1, 0).astype(BF16)
        kv_h = kv.reshape(-1, 2, kv_heads, head).transpose(1, 2, 0, 3)
        key_h, val_h = kv_h[0], kv_h[1]

        query = heads_of(dot(hid, w_q, 1, 0).astype(BF16))
        scale = head ** -0.5
        prob = jax.nn.softmax(bdot(query, key_h, 2, 2) * scale, axis=-1)
        prob_bf = prob.astype(BF16)
        ctx = flat_of(bdot(prob_bf, val_h, 2, 1).astype(BF16))
        mid = (hid.astype(F32) + dot(ctx, w_o, 1, 0)).astype(BF16)
        cm_all = gather(jnp.concatenate([ctx, mid], axis=1))
        ctx_all, mid_all = cm_all[:, :d_model], cm_all[:, d_model:]
        dec_act, dec_pull = jax.vjp(jax.nn.gelu, dot(mid, w_1, 1, 0))
        dec_act = dec_act.astype(BF16)
        dec_gact = dot(cot, w_2, 1, 1).astype(BF16)
        dec_gpre = dec_pull(dec_gact.astype(F32))[0].astype(BF16)
        g_mid = (cot.astype(F32) + dot(dec_gpre, w_1, 1, 1)).astype(BF16)
        g_ctx = heads_of(dot(g_mid, w_o, 1, 1).astype(BF16))
        g_prob = bdot(g_ctx, val_h, 2, 2)
        g_val = bdot(prob_bf, g_ctx, 1, 1).astype(BF16)
        g_logit = (prob * (g_prob - jnp.sum(prob * g_prob, axis=-1, keepdims=True)) * scale).astype(BF16)
        g_key = bdot(g_logit, query, 1, 1).astype(BF16)
        g_kv = jnp.concatenate([g_key[i] for i in range(kv_heads)] + [g_val[i] for i in range(kv_heads)], axis=1)
        g_mem = dot(g_kv, w_kv, 1, 1).astype(BF16)

        g_wkv = scatter(dot(memory, g_kv, 0, 0))
        g_down_own, g_mem, g_logit, g_mid, dec_gpre = lax.optimization_barrier((dot(act, g_mem, 0, 0), g_mem, g_logit, g_mid, dec_gpre))
        g_down = scatter(g_down_own)
        g_act = dot(g_mem, down, 1, 1).astype(BF16)
        g_pre = gelu_pull(g_act.astype(F32))[0].astype(BF16)
        g_up_own = with_layout_constraint(dot(x, g_pre, 0, 0), Layout((0, 1)))
        g_up_own, g_pre, g_logit, g_mid, dec_gpre = lax.optimization_barrier((g_up_own, g_pre, g_logit, g_mid, dec_gpre))
        g_up = scatter(g_up_own)

        g_query = flat_of(bdot(g_logit, key_h, 2, 1).astype(BF16))
        dh = (g_mid.astype(F32) + dot(g_query, w_q, 1, 1)).astype(BF16)
        dh = lax.ppermute(dh, 'stage', partner_perm)

        n1 = d_model // n_dev
        n2 = w_1.shape[1] // n_dev
        sent = [t.reshape(s_dec, n_dev, -1) for t in (dec_act, dec_gpre, g_mid, g_query)]
        cols = lax.all_to_all(jnp.concatenate(sent, axis=2), AXES, split_axis=1, concat_axis=0, tiled=True)
        cols = cols.reshape(n_dev * s_dec, -1)
        act_c, gpre_c, gmid_c, gq_c = (cols[:, :n2], cols[:, n2:2 * n2], cols[:, 2 * n2:2 * n2 + n1], cols[:, 2 * n2 + n1:])
        g_w2 = dot(act_c, cot_all, 0, 0)
        blocks = jnp.concatenate([dot(mid_all, gpre_c, 0, 0), dot(ctx_all, gmid_c, 0, 0), dot(hid_all, gq_c, 0, 0)], axis=1)
        blocks = lax.all_to_all(blocks.reshape(n_dev, n1, -1), AXES, split_axis=0, concat_axis=0, tiled=True)
        g_w1, g_wo, g_wq = (b.transpose(1, 0, 2).reshape(n1, -1) for b in (blocks[:, :, :n2], blocks[:, :, n2:n2 + n1], blocks[:, :, n2 + n1:]))
        dx = (g_mem.astype(F32) + dot(g_pre, up, 1, 1)).astype(BF16)
        g_wk = g_wkv[:, :kv_width].reshape(1, n1, kv_heads, head)
        g_wv = g_wkv[:, kv_width:].reshape(1, n1, kv_heads, head)
        return (dx[None], dh[None], g_up[None], g_down[None], g_wk, g_wv, g_wq[None], g_wo[None], g_w1[None], g_w2[None])

    return jax.shard_map(step, mesh=mesh,
                         in_specs=(row_spec, row_spec, row_spec, full_spec3, full_spec3, full_spec4, full_spec4, full_spec3, full_spec3, full_spec3, full_spec3),
                         out_specs=(row_spec, row_spec, grad_spec3, grad_spec3, grad_spec4, grad_spec4, grad_spec3, grad_spec3, grad_spec3, grad_spec3),
                         check_vma=False)
```

time: 1920 us -> 1030 us (0.54)
  waiting for transfers between devices: 1240 us -> 463 us
  local copies, waits for them, and re-layouts: 153 us -> 52.7 us
  matrix products: 497 us -> 468 us
    reduce_scatter x4 -> x3, waiting for transfers between devices: 895 us -> 404 us  [scatter(): return lax.psum_scatter(own, AXES, scatter_dimension=0, tiled=True)]
    unnamed x8 -> x5, waiting for transfers between devices: 311 us -> 0.6 us
    another operation x6 -> x5, local copies, waits for them, and re-layouts: 134 us -> 8.31 us  [the longest x1 5.71 us: step(): g_w1[None]]
    all_to_all x0 -> x2, waiting for transfers between devices: none -> 59.2 us  [the longest x1 30.6 us: step(): lax.all_to_all(blocks.reshape(n_dev, n1, -1), AXES, split_axis=0, concat_...]
    dot_general x29 -> x24, matrix products: 497 us -> 458 us  [the longest x20 450 us: dot(): lax.dot_general(lhs, rhs, (((lhs_dim,), (rhs_dim,)), ((), ())), preferred...]
    ppermute x4 -> x2, waiting for transfers between devices: 29.1 us -> 0.01 us  [the longest x1 0.01 us: step(): lax.ppermute(jnp.concatenate([h_dec[0], cot_out[0]], axis=1), 'stage', pa...]
  transfers between devices with their start and end apart: 10 -> 9, of which waited for: 7 -> 4; matrix products, arithmetic and copies ran while one was open for 20% -> 45% of each run, Pallas kernels for 0% -> 0%
where the time goes in v1:
time: 1030 us; the launch traced here: 1020 us
  matrix products  468 us (45%)
  waiting for transfers between devices  463 us (45%)
  local copies, waits for them, and re-layouts  52.7 us (5%)
  between operations  14.4 us (1%)
  starting transfers between devices  12.3 us (1%)
    dot_general x20, matrix products, dot(): lax.dot_general(lhs, rhs, (((lhs_dim,), (rhs_dim,)), ((), ())), preferred...  450 us
    reduce_scatter x3, waiting for transfers between devices, scatter(): return lax.psum_scatter(own, AXES, scatter_dimension=0, tiled=True)  404 us
    all_to_all x1, waiting for transfers between devices, step(): lax.all_to_all(blocks.reshape(n_dev, n1, -1), AXES, split_axis=0, concat_...  30.6 us
    all_to_all x1, waiting for transfers between devices, step(): lax.all_to_all(jnp.concatenate(sent, axis=2), AXES, split_axis=1, concat_...  28.7 us
  transfers between devices with their start and end apart: 9, of which 4 were waited for; matrix products, arithmetic and copies ran while one was open for 45% of the time, Pallas kernels for 0%

profile of v1, /device:TPU:0, one launch (start us, length us, event | category | flops | bytes accessed | tf_op | source)
XLA Modules:
  0.0 1016.2 jit_solution(5954747965694655207)
XLA Ops:
  13.5 50.9 %fusion.23 = f32[1536,8960]{1,0:T(8,128)} fusion(bf16[1,1536,8960]{2,1,0:T(8,128)(2,1)} %param.14, bf16[1,1536,1536]{2,1,0:T(8,128)(2,1)} %param.11), kind=kOutput, calls=%fused_computation.30 | convolution fusion | flops 42278584320 | bytes 87293952 | tf_op jit(solution)/shard_map/dot_general | solution.py:14
  64.6 60.0 %add_convert_fusion.1 = bf16[1536,1536]{1,0:T(8,128)(2,1)} fusion(bf16[1,8960,1536]{2,1,0:T(8,128)(2,1)} %param.15, bf16[1,1536,1536]{2,1,0:T(8,128)(2,1)} %param.11, f32[1536,8960]{1,0:T(8,128)} %fusion.23), kind=kOutput, calls=%fused_computation.35 | convolution fusion | flops 42409525248 | bytes 92012544 | tf_op jit(solution)/shard_map/dot_general | solution.py:14
  124.6 5.0 convolution_convert_fusion.2
  144.3 15.1 %multiply_convert_fusion.2 = (bf16[64,8960]{1,0:T(8,128)(2,1)}, f32[64,8960]{1,0:T(8,128)S(1)}) fusion(bf16[64,1536]{1,0:T(8,128)(2,1)S(1)} %add_convert_fusion.3, bf16[1,1536,8960]{2,1,0:T(8,128)(2,1)} %param.20), kind=kOutput, calls=%fused_computation.82 | convolution fusion | flops 1766768640 | bytes 31162368 | tf_op jit(solution)/shard_map/dot_general | solution.py:14
  159.4 13.8 %fusion.78 = bf16[64,8960]{1,0:T(8,128)(2,1)S(1)} fusion(f32[64,8960]{1,0:T(8,128)S(1)} %get-tuple-element.43, bf16[1,8960,1536]{2,1,0:T(8,128)(2,1)} %param.21, bf16[64,3072]{1,0:T(8,128)(2,1)} %collective-permute-done), kind=kOutput, calls=%fused_computation.81 | convolution fusion | flops 1774223360 | bytes 31162368 | tf_op jit(solution)/shard_map/dot_general | solution.py:14
  173.2 14.5 %add_convert_fusion.2 = (bf16[64,1536]{1,0:T(8,128)(2,1)}, f32[64,1536]{1,0:T(8,128)S(1)}) fusion(bf16[64,3072]{1,0:T(8,128)(2,1)} %collective-permute-done, bf16[64,8960]{1,0:T(8,128)(2,1)S(1)} %fusion.78, bf16[1,1536,8960]{2,1,0:T(8,128)(2,1)} %param.20), kind=kOutput, calls=%fused_computation.106 | convolution fusion | flops 1761902592 | bytes 29458432 | tf_op jit(solution)/shard_map/dot_general | solution.py:14
  187.7 4.0 fusion.69
  192.1 5.8 multiply_convert_fusion.1
  208.7 58.0 %fusion.110 = f32[8960,1536]{1,0:T(8,128)} fusion(bf16[1536,1536]{1,0:T(8,128)(2,1)S(1)} %convolution_convert_fusion.1, f32[1536,8960]{1,0:T(8,128)} %fusion.23), kind=kOutput, calls=%fused_computation.119 | convolution fusion | flops 42402447360 | bytes 114819072 | tf_op jit(solution)/shard_map/dot_general | solution.py:14
  267.4 6.7 fusion.93
  274.2 81.1 %fusion.4 = bf16[1536,8960]{1,0:T(8,128)(2,1)} fusion(f32[1536,8960]{1,0:T(8,128)} %fusion.23, bf16[1536,1536]{1,0:T(8,128)(2,1)} %copy-done.16, bf16[1,8960,1536]{2,1,0:T(8,128)(2,1)} %param.15), kind=kOutput, calls=%fused_computation.8 | convolution fusion | flops 42581360640 | bytes 114819072 | tf_op jit(solution)/shard_map/dot_general | solution.py:14
  355.3 51.3 %convolution_bitcast_fusion = f32[1536,8960]{1,0:T(8,128)} fusion(bf16[1536,8960]{1,0:T(8,128)(2,1)} %fusion.4, bf16[1,1536,1536]{2,1,0:T(8,128)(2,1)} %param.11), kind=kOutput, calls=%fused_computation.17 | convolution fusion | flops 42278584320 | bytes 87293952 | tf_op jit(solution)/shard_map/dot_general | solution.py:14
  418.6 6.1 concatenate.22
  427.9 5.7 fusion.63
  435.5 28.7 %all-to-all-done = bf16[64,16,1312]{2,0,1:T(8,128)(2,1)S(1)} async-done(((bf16[64,16,1312]{2,0,1:T(8,128)(2,1)}), bf16[64,16,1312]{2,0,1:T(8,128)(2,1)S(1)}, u32[]{:S(2)}, u32[]{:S(2)}) %all-to-all-start) | async-done | bytes 2687008 | tf_op jit(solution)/shard_map/all_to_all | solution.py:105
  478.4 6.7 copy.54
  485.1 4.0 all-to-all-start.1
  489.2 58.4 %fusion.35 = bf16[1,1536,1536]{2,1,0:T(8,128)(2,1)} fusion(bf16[1536,8960]{1,0:T(8,128)(2,1)} %fusion.4, bf16[1,1536,8960]{2,1,0:T(8,128)(2,1)} %param.14, bf16[1536,1536]{1,0:T(8,128)(2,1)} %copy-done.16), kind=kOutput, calls=%fused_computation.37 | convolution fusion | flops 42285662208 | bytes 64487424 | tf_op jit(solution)/shard_map/dot_general | solution.py:14
  549.9 5.8 convolution_bitcast_fusion.1
  555.7 30.6 %all-to-all-done.1 = f32[16,96,752]{2,1,0:T(8,128)} async-done(((f32[16,96,752]{2,1,0:T(8,128)}), f32[16,96,752]{2,1,0:T(8,128)}, u32[]{:S(2)}, u32[]{:S(2)}) %all-to-all-start.1) | async-done | bytes 4620320 | tf_op jit(solution)/shard_map/all_to_all | solution.py:110
  594.4 4.2 copy.57
  598.6 5.7 broadcast_in_dim_reshape.11
  604.3 130.3 %reduce-scatter.4.cloned.1.call-done = f32[96,8960]{1,0:T(8,128)} async-done(((f32[1536,8960]{1,0:T(8,128)}), f32[96,8960]{1,0:T(8,128)}) %reduce-scatter.4.cloned.1.call-update) | async-done | bytes 3440656 | tf_op jit(solution)/shard_map/reduce_scatter | solution.py:26
  734.6 273.2 %reduce-scatter.6.cloned.1.call-done = f32[560,1536]{1,0:T(8,128)} async-done(((f32[8960,1536]{1,0:T(8,128)}), f32[560,1536]{1,0:T(8,128)}) %reduce-scatter.6.cloned.1.call-update) | async-done | bytes 3440656 | tf_op jit(solution)/shard_map/reduce_scatter | solution.py:26
  (96 shorter events, 76.2 us)
Async XLA Ops:
  7.2 457.0 %all-gather.5.cloned.1.call-start = ((), (), s32[]{:S(2)}) async-start(), calls=%async_computation.9 | async-start | bytes 6684672 | tf_op jit(solution)/shard_map/all_gather | solution.py:22
  9.0 121.5 %collective-permute-start = (bf16[64,3072]{1,0:T(8,128)(2,1)}, bf16[64,3072]{1,0:T(8,128)(2,1)}, u32[]{:S(2)}, u32[]{:S(2)}) collective-permute-start(bf16[64,3072]{1,0:T(8,128)(2,1)} %pad_maximum_fusion.2), channel_id=1, source_target_pairs={{0,4},{1,5},{2,6},{3,7},{4,0},{5,1},{6,2},{7,3},{8,12},{9,13},{10,... | collective-permute-start | bytes 1179656 | tf_op jit(solution)/shard_map/ppermute | solution.py:48
  13.5 51.0 %copy-start.12 = (bf16[1,1536,2,128]{3,2,1,0:T(2,128)(2,1)S(1)}, bf16[1,1536,2,128]{3,2,1,0:T(2,128)(2,1)}, u32[]{:S(2)}) copy-start(bf16[1,1536,2,128]{3,2,1,0:T(2,128)(2,1)} %param.17) | copy-start | bytes 2359300
  64.6 60.0 %copy-start.13 = (bf16[1536,512]{1,0:T(8,128)(2,1)}, bf16[1536,512]{1,0:T(8,128)(2,1)S(1)}, u32[]{:S(2)}) copy-start(bf16[1536,512]{1,0:T(8,128)(2,1)S(1)} %bitcast_dynamic-update-slice_fusion) | copy-start | bytes 4718596
  130.5 7.9 copy-start.9
  134.7 5.8 copy-start.10
  140.9 18.5 %copy-start.7 = (bf16[64,1536]{1,0:T(8,128)(2,1)}, bf16[64,1536]{1,0:T(8,128)(2,1)S(1)}, u32[]{:S(2)}) copy-start(bf16[64,1536]{1,0:T(8,128)(2,1)S(1)} %reshape.76) | copy-start | bytes 589828
  144.3 15.1 %copy-start.4 = (bf16[64,1536]{1,0:T(8,128)(2,1)}, bf16[64,1536]{1,0:T(8,128)(2,1)S(1)}, u32[]{:S(2)}) copy-start(bf16[64,1536]{1,0:T(8,128)(2,1)S(1)} %add_convert_fusion.3) | copy-start | bytes 589828
  173.2 14.6 %copy-start = (bf16[64,8960]{1,0:T(8,128)(2,1)}, bf16[64,8960]{1,0:T(8,128)(2,1)S(1)}, u32[]{:S(2)}) copy-start(bf16[64,8960]{1,0:T(8,128)(2,1)S(1)} %fusion.78) | copy-start | bytes 3440644
  192.1 275.6 %all-gather.3.cloned.1.call-start = ((), (), s32[]{:S(2)}) async-start(), calls=%async_computation.8 | async-start | bytes 6684672 | tf_op jit(solution)/shard_map/all_gather | solution.py:22
  192.1 5.9 copy-start.11
  198.0 3.8 copy-start.2
  206.6 2.1 copy-start.16
  208.7 58.0 %copy-start.5 = (bf16[64,1536]{1,0:T(8,128)(2,1)S(1)}, bf16[64,1536]{1,0:T(8,128)(2,1)}, u32[]{:S(2)}) copy-start(bf16[64,1536]{1,0:T(8,128)(2,1)} %copy-done.4) | copy-start | bytes 589828
  208.7 58.0 %copy-start.8 = (bf16[64,1536]{1,0:T(8,128)(2,1)S(1)}, bf16[64,1536]{1,0:T(8,128)(2,1)}, u32[]{:S(2)}) copy-start(bf16[64,1536]{1,0:T(8,128)(2,1)} %copy-done.7) | copy-start | bytes 589828
  274.1 273.4 %reduce-scatter.8.cloned.1.call-start = ((), (), s32[]{:S(2)}) async-start(), calls=%async_computation.7 | async-start | bytes 3342336 | tf_op jit(solution)/shard_map/reduce_scatter | solution.py:26
  355.3 379.3 %reduce-scatter.4.cloned.1.call-start = ((), (), s32[]{:S(2)}) async-start(), calls=%async_computation.5 | async-start | bytes 58490880 | tf_op jit(solution)/shard_map/reduce_scatter | solution.py:26
  406.7 601.1 %reduce-scatter.6.cloned.1.call-start = ((), (), s32[]{:S(2)}) async-start(), calls=%async_computation.6 | async-start | bytes 58490880 | tf_op jit(solution)/shard_map/reduce_scatter | solution.py:26
  408.3 6.4 copy-start.1
  410.5 7.5 copy-start.6
  424.7 39.5 %all-to-all-start = ((bf16[64,16,1312]{2,0,1:T(8,128)(2,1)}), bf16[64,16,1312]{2,0,1:T(8,128)(2,1)S(1)}, u32[]{:S(2)}, u32[]{:S(2)}) async-start(bf16[64,16,1312]{2,0,1:T(8,128)(2,1)} %concatenate.22), calls=%async_computation.3 | async-start | bytes 5767168 | tf_op jit(solution)/shard_map/all_to_all | solution.py:105
  433.6 114.0 %collective-permute-start.1 = (bf16[64,1536]{1,0:T(8,128)(2,1)}, bf16[64,1536]{1,0:T(8,128)(2,1)}, u32[]{:S(2)}, u32[]{:S(2)}) collective-permute-start(bf16[64,1536]{1,0:T(8,128)(2,1)} %fusion.63), channel_id=1, source_target_pairs={{0,4},{1,5},{2,6},{3,7},{4,0},{5,1},{6,2},{7,3},{8,12},{9,13},{10,... | collective-permute-start | bytes 589832 | tf_op jit(solution)/shard_map/ppermute | solution.py:100
  467.6 5.6 copy-start.15
  485.1 101.1 %all-to-all-start.1 = ((f32[16,96,752]{2,1,0:T(8,128)}), f32[16,96,752]{2,1,0:T(8,128)}, u32[]{:S(2)}, u32[]{:S(2)}) async-start(f32[16,96,752]{2,1,0:T(8,128)} %bitcast.166), calls=%async_computation.4 | async-start | bytes 9437184 | tf_op jit(solution)/shard_map/all_to_all | solution.py:110
  (2 other events, 3.1 us)
Sparse Core Ops, SparseCore 0:
  192.2 42.2 all-gather.4
  274.3 42.2 all-gather.2
  355.4 54.6 reduce-scatter.7
  415.8 318.7 reduce-scatter.3
  740.3 267.4 reduce-scatter.5

commit v2 on v1

--- a/solution.py
+++ b/solution.py
@@ -7,7 +7,8 @@
 
 F32 = jnp.float32
 BF16 = jnp.bfloat16
-AXES = ('data', 'stage')
+AXES = ('data', 'chip', 'core')
+CHIPS = ('data', 'chip')
 
 
 def dot(lhs, rhs, lhs_dim, rhs_dim):
@@ -23,13 +24,14 @@
 
 
 def scatter(own):
-    return lax.psum_scatter(own, AXES, scatter_dimension=0, tiled=True)
+    return lax.psum_scatter(own, CHIPS, scatter_dimension=0, tiled=True)
 
 
 def solution(mesh):
-    stage_size = mesh.shape['stage']
-    n_dev = mesh.shape['data'] * stage_size
-    partner_perm = [(index, (index + stage_size // 2) % stage_size) for index in range(stage_size)]
+    n_data, chips = mesh.shape['data'], mesh.shape['stage'] // 2
+    n_dev = n_data * chips * 2
+    mesh = jax.sharding.Mesh(mesh.devices.reshape(n_data, chips, 2), AXES)
+    partner_perm = [(index, (index + chips // 2) % chips) for index in range(chips)]
     row_spec = P(AXES, None, None)
     full_spec3 = P(None, None, None)
     full_spec4 = P(None, None, None, None)
@@ -45,7 +47,7 @@
         w_q, w_o, w_1, w_2 = w_query[0], w_out[0], w_ff1[0], w_ff2[0]
         w_kv = jnp.concatenate([w_key[0].reshape(d_model, kv_width), w_val[0].reshape(d_model, kv_width)], axis=1)
 
-        hg = lax.ppermute(jnp.concatenate([h_dec[0], cot_out[0]], axis=1), 'stage', partner_perm)
+        hg = lax.ppermute(jnp.concatenate([h_dec[0], cot_out[0]], axis=1), 'chip', partner_perm)
         hid, cot = hg[:, :d_model], hg[:, d_model:]
         hg_all = gather(hg)
         hid_all, cot_all = hg_all[:, :d_model], hg_all[:, d_model:]
@@ -57,10 +59,24 @@
         def flat_of(heads):
             return heads.reshape(kv_heads, group, s_dec, head).transpose(2, 0, 1, 3).reshape(s_dec, d_model)
 
+        core = lax.axis_index('core')
+
+        def swap(own):
+            return lax.ppermute(own, 'core', [(0, 1), (1, 0)])
+
+        def half(arr, axis, index):
+            size = arr.shape[axis] // 2
+            return lax.dynamic_slice_in_dim(arr, index.astype(jnp.uint32) * size, size, axis)
+
+        def join(own, other):
+            return jnp.where(core == 0, jnp.concatenate([own, other], axis=1), jnp.concatenate([other, own], axis=1))
+
+        x_sib = swap(x)
         pre = dot(x, up, 1, 0)
-        act, gelu_pull = jax.vjp(jax.nn.gelu, pre)
-        act = act.astype(BF16)
+        act = lax.optimization_barrier(jax.nn.gelu(pre).astype(BF16))
+        act_sib = swap(act)
         memory = (x.astype(F32) + dot(act, down, 1, 0)).astype(BF16)
+        mem_sib = swap(memory)
         kv = dot(memory, w_kv, 1, 0).astype(BF16)
         kv_h = kv.reshape(-1, 2, kv_heads, head).transpose(1, 2, 0, 3)
         key_h, val_h = kv_h[0], kv_h[1]
@@ -77,6 +93,7 @@
         dec_act = dec_act.astype(BF16)
         dec_gact = dot(cot, w_2, 1, 1).astype(BF16)
         dec_gpre = dec_pull(dec_gact.astype(F32))[0].astype(BF16)
+        gpre_all = gather(dec_gpre)
         g_mid = (cot.astype(F32) + dot(dec_gpre, w_1, 1, 1)).astype(BF16)
         g_ctx = heads_of(dot(g_mid, w_o, 1, 1).astype(BF16))
         g_prob = bdot(g_ctx, val_h, 2, 2)
@@ -86,30 +103,50 @@
         g_kv = jnp.concatenate([g_key[i] for i in range(kv_heads)] + [g_val[i] for i in range(kv_heads)], axis=1)
         g_mem = dot(g_kv, w_kv, 1, 1).astype(BF16)
 
-        g_wkv = scatter(dot(memory, g_kv, 0, 0))
-        g_down_own, g_mem, g_logit, g_mid, dec_gpre = lax.optimization_barrier((dot(act, g_mem, 0, 0), g_mem, g_logit, g_mid, dec_gpre))
-        g_down = scatter(g_down_own)
-        g_act = dot(g_mem, down, 1, 1).astype(BF16)
-        g_pre = gelu_pull(g_act.astype(F32))[0].astype(BF16)
-        g_up_own = with_layout_constraint(dot(x, g_pre, 0, 0), Layout((0, 1)))
-        g_up_own, g_pre, g_logit, g_mid, dec_gpre = lax.optimization_barrier((g_up_own, g_pre, g_logit, g_mid, dec_gpre))
-        g_up = scatter(g_up_own)
+        kv_sib = swap(g_kv)
+        gm_sib = dot(kv_sib, half(w_kv, 0, core), 1, 1).astype(BF16)
+        own = lax.optimization_barrier(dot(act, half(g_mem, 1, core), 0, 0))
+        down_half = own + dot(act_sib, gm_sib, 0, 0)
+        down_half, g_mem, g_logit, g_mid, dec_gpre, kv_sib, mem_sib = lax.optimization_barrier((down_half, g_mem, g_logit, g_mid, dec_gpre, kv_sib, mem_sib))
+        down_sum = scatter(down_half)
+
+        def gpre_half(index):
+            g_act = dot(g_mem, half(down, 0, index), 1, 1).astype(BF16)
+            return jax.vjp(jax.nn.gelu, half(pre, 1, index))[1](g_act.astype(F32))[0].astype(BF16)
+
+        gpre_send = gpre_half(1 - core)
+        gpre_sib = swap(gpre_send)
+        gpre_own = gpre_half(core)
+        wkv_half = dot(memory, half(g_kv, 1, core), 0, 0) + dot(mem_sib, half(kv_sib, 1, core), 0, 0)
+        own = lax.optimization_barrier(dot(x, gpre_own, 0, 0))
+        up_half = with_layout_constraint(own + dot(x_sib, gpre_sib, 0, 0), Layout((0, 1)))
+        up_half = with_layout_constraint(jnp.concatenate([up_half, wkv_half], axis=1), Layout((0, 1)))
+        up_half, gpre_own, g_logit, g_mid, dec_gpre = lax.optimization_barrier((up_half, gpre_own, g_logit, g_mid, dec_gpre))
+        up_sum = scatter(up_half)
+        n1 = d_model // n_dev
+        n2 = w_1.shape[1] // n_dev
+        g_down = join(half(down_sum, 0, core), swap(half(down_sum, 0, 1 - core)))
+        up_own, up_other = half(up_sum, 0, core), swap(half(up_sum, 0, 1 - core))
+        n_ff = up_own.shape[1] - kv_width
+        g_up = join(up_own[:, :n_ff], up_other[:, :n_ff])
+        g_wkv = join(up_own[:, n_ff:], up_other[:, n_ff:])
 
         g_query = flat_of(bdot(g_logit, key_h, 2, 1).astype(BF16))
         dh = (g_mid.astype(F32) + dot(g_query, w_q, 1, 1)).astype(BF16)
-        dh = lax.ppermute(dh, 'stage', partner_perm)
+        dh = lax.ppermute(dh, 'chip', partner_perm)
 
-        n1 = d_model // n_dev
-        n2 = w_1.shape[1] // n_dev
-        sent = [t.reshape(s_dec, n_dev, -1) for t in (dec_act, dec_gpre, g_mid, g_query)]
+        sent = [t.reshape(s_dec, n_dev, -1) for t in (dec_act, g_mid, g_query)]
         cols = lax.all_to_all(jnp.concatenate(sent, axis=2), AXES, split_axis=1, concat_axis=0, tiled=True)
         cols = cols.reshape(n_dev * s_dec, -1)
-        act_c, gpre_c, gmid_c, gq_c = (cols[:, :n2], cols[:, n2:2 * n2], cols[:, 2 * n2:2 * n2 + n1], cols[:, 2 * n2 + n1:])
+        act_c, gmid_c, gq_c = cols[:, :n2], cols[:, n2:n2 + n1], cols[:, n2 + n1:]
         g_w2 = dot(act_c, cot_all, 0, 0)
-        blocks = jnp.concatenate([dot(mid_all, gpre_c, 0, 0), dot(ctx_all, gmid_c, 0, 0), dot(hid_all, gq_c, 0, 0)], axis=1)
+        mid_c = lax.dynamic_slice_in_dim(mid_all, lax.axis_index(AXES) * n1, n1, 1)
+        g_w1 = dot(mid_c, gpre_all, 0, 0)
+        blocks = jnp.concatenate([dot(ctx_all, gmid_c, 0, 0), dot(hid_all, gq_c, 0, 0)], axis=1)
         blocks = lax.all_to_all(blocks.reshape(n_dev, n1, -1), AXES, split_axis=0, concat_axis=0, tiled=True)
-        g_w1, g_wo, g_wq = (b.transpose(1, 0, 2).reshape(n1, -1) for b in (blocks[:, :, :n2], blocks[:, :, n2:n2 + n1], blocks[:, :, n2 + n1:]))
-        dx = (g_mem.astype(F32) + dot(g_pre, up, 1, 1)).astype(BF16)
+        g_wo, g_wq = (b.transpose(1, 0, 2).reshape(n1, -1) for b in (blocks[:, :, :n1], blocks[:, :, n1:]))
+        part = lax.optimization_barrier(dot(gpre_own, half(up, 1, core), 1, 1))
+        dx = (g_mem.astype(F32) + part + dot(gpre_send, half(up, 1, 1 - core), 1, 1)).astype(BF16)
         g_wk = g_wkv[:, :kv_width].reshape(1, n1, kv_heads, head)
         g_wv = g_wkv[:, kv_width:].reshape(1, n1, kv_heads, head)
         return (dx[None], dh[None], g_up[None], g_down[None], g_wk, g_wv, g_wq[None], g_wo[None], g_w1[None], g_w2[None])

time: 1030 us -> 818 us (0.79)
  waiting for transfers between devices: 463 us -> 187 us
  matrix products: 468 us -> 529 us
  other arithmetic: 5.48 us -> 30.6 us
  local copies, waits for them, and re-layouts: 52.7 us -> 34.2 us
    reduce_scatter x3 -> x2, waiting for transfers between devices: 404 us -> 187 us  [scatter(): return lax.psum_scatter(own, CHIPS, scatter_dimension=0, tiled=True)]
    dot_general x20 -> x25, matrix products: 450 us -> 513 us  [dot(): lax.dot_general(lhs, rhs, (((lhs_dim,), (rhs_dim,)), ((), ())), preferred...]
    all_to_all x1, waiting for transfers between devices: 30.6 us -> 0.01 us  [step(): lax.all_to_all(blocks.reshape(n_dev, n1, -1), AXES, split_axis=0, concat_...]
    all_to_all x1, waiting for transfers between devices: 28.7 us -> 0.01 us  [step(): lax.all_to_all(jnp.concatenate(sent, axis=2), AXES, split_axis=1, concat_...]
    concatenate x1 -> x4, other arithmetic: 2.91 us -> 21.5 us  [the longest x1 19.8 us: step(): jnp.concatenate([up_half, wkv_half], axis=1)]
  transfers between devices with their start and end apart: 9 -> 16, of which waited for: 4 -> 1; matrix products, arithmetic and copies ran while one was open for 45% -> 70% of each run, Pallas kernels for 0% -> 0%
where the time goes in v2:
time: 818 us; the launch traced here: 812 us
  matrix products  529 us (65%)
  waiting for transfers between devices  187 us (23%)
  local copies, waits for them, and re-layouts  34.2 us (4%)
  other arithmetic  30.6 us (4%)
  between operations  15.8 us (2%)
  starting transfers between devices  15.1 us (2%)
    dot_general x25, matrix products, dot(): lax.dot_general(lhs, rhs, (((lhs_dim,), (rhs_dim,)), ((), ())), preferred...  513 us
    reduce_scatter x2, waiting for transfers between devices, scatter(): return lax.psum_scatter(own, CHIPS, scatter_dimension=0, tiled=True)  187 us
    concatenate x1, other arithmetic, step(): jnp.concatenate([up_half, wkv_half], axis=1)  19.8 us
  transfers between devices with their start and end apart: 16, of which 1 were waited for; matrix products, arithmetic and copies ran while one was open for 70% of the time, Pallas kernels for 0%

profile of v2, /device:TPU:0, one launch (start us, length us, event | category | flops | bytes accessed | tf_op | source)
XLA Modules:
  0.0 811.8 jit_solution(14147718904183257593)
XLA Ops:
  13.1 61.4 %fusion.9 = (bf16[1536,8960]{1,0:T(8,128)(2,1)}, f32[1536,8960]{1,0:T(8,128)}) fusion(bf16[1,1536,8960]{2,1,0:T(8,128)(2,1)} %param.14, bf16[1,1536,1536]{2,1,0:T(8,128)(2,1)} %param.11), kind=kOutput, calls=%fused_computation.10 | convolution fusion | flops 42402447360 | bytes 114819072 | tf_op jit(solution)/shard_map/dot_general | solution.py:15
  75.5 55.6 %add_convert_fusion.1 = bf16[1536,1536]{1,0:T(8,128)(2,1)} fusion(bf16[1536,8960]{1,0:T(8,128)(2,1)} %get-tuple-element.50, bf16[1,8960,1536]{2,1,0:T(8,128)(2,1)} %param.15, bf16[1,1536,1536]{2,1,0:T(8,128)(2,1)} %param.11), kind=kOutput, calls=%fused_computation.69 | convolution fusion | flops 42285662208 | bytes 64487424 | tf_op jit(solution)/shard_map/dot_general | solution.py:15
  132.0 5.5 convolution_convert_fusion.4
  153.2 15.5 %multiply_convert_fusion.1 = (bf16[64,8960]{1,0:T(8,128)(2,1)}, f32[64,8960]{1,0:T(8,128)S(1)}) fusion(bf16[64,1536]{1,0:T(8,128)(2,1)S(1)} %add_convert_fusion.3, bf16[1,1536,8960]{2,1,0:T(8,128)(2,1)} %param.20), kind=kOutput, calls=%fused_computation.116 | convolution fusion | flops 1766768640 | bytes 31162368 | tf_op jit(solution)/shard_map/dot_general | solution.py:15
  168.7 14.4 %fusion.97 = bf16[64,8960]{1,0:T(8,128)(2,1)} fusion(f32[64,8960]{1,0:T(8,128)S(1)} %get-tuple-element.57, bf16[1,8960,1536]{2,1,0:T(8,128)(2,1)} %param.21, bf16[64,3072]{1,0:T(8,128)(2,1)} %collective-permute-done), kind=kOutput, calls=%fused_computation.115 | convolution fusion | flops 1774223360 | bytes 31162368 | tf_op jit(solution)/shard_map/dot_general | solution.py:15
  183.7 14.8 %add_convert_fusion.2 = (bf16[64,1536]{1,0:T(8,128)(2,1)}, f32[64,1536]{1,0:T(8,128)S(1)}) fusion(bf16[64,3072]{1,0:T(8,128)(2,1)} %collective-permute-done, bf16[64,8960]{1,0:T(8,128)(2,1)} %fusion.97, bf16[1,1536,8960]{2,1,0:T(8,128)(2,1)} %param.20), kind=kOutput, calls=%fused_computation.146 | convolution fusion | flops 1761902592 | bytes 29458432 | tf_op jit(solution)/shard_map/dot_general | solution.py:15
  198.5 4.1 fusion.88
  205.0 6.2 multiply_convert_fusion
  212.9 4.8 convolution_convert_fusion.2
  217.7 30.8 %fusion.76 = f32[8960,768]{1,0:T(8,128)} fusion(bf16[1536,8960]{1,0:T(8,128)(2,1)} %get-tuple-element.50, bf16[1536,1536]{1,0:T(8,128)(2,1)S(1)} %convolution_convert_fusion.2, u32[]{:T(128)S(6)} %mul.215), kind=kOutput, calls=%fused_computation.101 | convolution fusion | flops 21139292160 | bytes 57409540 | tf_op jit(solution)/shard_map/dot_general | solution.py:15
  249.7 37.4 %convolution_add_fusion = f32[8960,768]{1,0:T(8,128)} fusion(f32[8960,768]{1,0:T(8,128)} %fusion.76, bf16[1536,8960]{1,0:T(8,128)(2,1)} %collective-permute-done.1, bf16[1536,512]{0,1:T(8,128)(2,1)} %copy-done.14, bf16[1536,512]{1,0:T(8,128)(2,1)} %bitcast_dynamic-update-slice_fusion, u32[]{:T(128)S(6)} %mul.215), kind=kOutput, calls=%fused_computation.54 | convolution fusion | flops 22355312640 | bytes 84934656 | tf_op jit(solution)/shard_map/dot_general | solution.py:15
  288.6 5.0 fusion.108
  293.6 47.3 %fusion.17 = bf16[1536,4480]{1,0:T(8,128)(2,1)} fusion(f32[1536,8960]{1,0:T(8,128)} %get-tuple-element.51, u32[]{:T(128)S(6)} %mul.230, bf16[1536,1536]{1,0:T(8,128)(2,1)} %copy-done.17, bf16[1,8960,1536]{2,1,0:T(8,128)(2,1)} %param.15), kind=kOutput, calls=%fused_computation.27 | convolution fusion | flops 21290680320 | bytes 59769856 | tf_op jit(solution)/shard_map/dot_general | solution.py:15
  341.8 48.0 %fusion.12 = bf16[1536,4480]{1,0:T(8,128)(2,1)} fusion(f32[1536,8960]{1,0:T(8,128)} %get-tuple-element.51, u32[]{:T(128)S(6)} %mul.216, bf16[1536,1536]{1,0:T(8,128)(2,1)} %copy-done.17, bf16[1,8960,1536]{2,1,0:T(8,128)(2,1)} %param.15), kind=kOutput, calls=%fused_computation.22 | convolution fusion | flops 21290680320 | bytes 59769856 | tf_op jit(solution)/shard_map/dot_general | solution.py:15
  389.8 30.6 %convolution_bitcast_fusion = f32[1536,4480]{1,0:T(8,128)} fusion(bf16[1536,4480]{1,0:T(8,128)(2,1)} %fusion.12, bf16[1,1536,1536]{2,1,0:T(8,128)(2,1)} %param.11), kind=kOutput, calls=%fused_computation.51 | convolution fusion | flops 21139292160 | bytes 46006272 | tf_op jit(solution)/shard_map/dot_general | solution.py:15
  424.2 36.1 %bitcast_add_fusion = f32[1536,4480]{1,0:T(8,128)} fusion(f32[1536,4480]{1,0:T(8,128)} %convolution_bitcast_fusion, bf16[1536,4480]{1,0:T(8,128)(2,1)} %collective-permute-done.4, bf16[1536,1536]{1,0:T(8,128)(2,1)} %collective-permute-done.5), kind=kOutput, calls=%fused_computation.40 | convolution fusion | flops 21146173440 | bytes 73531392 | tf_op jit(solution)/shard_map/dot_general | solution.py:15
  460.3 19.8 %pad_maximum_fusion = f32[1536,4736]{1,0:T(8,128)} fusion(f32[1536,256]{1,0:T(8,128)S(1)} %convolution_add_fusion.1, f32[1536,4480]{1,0:T(8,128)} %bitcast_add_fusion), kind=kLoop, calls=%fused_computation.19 | loop fusion | flops 7274496 | bytes 58195968 | tf_op jit(solution)/shard_map/concatenate | solution.py:123
  487.7 12.1 %convolution_bitcast_fusion.1 = f32[1,96,8960]{2,1,0:T(8,128)} fusion(bf16[1024,8960]{1,0:T(8,128)(2,1)} %all-gather.8.cloned.1.call-done, bf16[1024,1536]{1,0:T(8,128)(2,1)} %slice.110, s32[]{:T(128)S(6)} %select_n.47), kind=kOutput, calls=%fused_computation.65 | convolution fusion | flops 1761607680 | bytes 22052868 | tf_op jit(solution)/shard_map/dot_general | solution.py:15
  507.0 4.5 fusion.82
  513.5 30.9 %fusion.42 = f32[1536,1536]{1,0:T(8,128)} fusion(bf16[1536,4480]{1,0:T(8,128)(2,1)} %fusion.12, bf16[1,1536,8960]{2,1,0:T(8,128)(2,1)} %param.14, u32[]{:T(128)S(6)} %mul.216), kind=kOutput, calls=%fused_computation.57 | convolution fusion | flops 21139292160 | bytes 36962308 | tf_op jit(solution)/shard_map/dot_general | solution.py:15
  560.0 186.9 %reduce-scatter.3.cloned.1.call-done = f32[192,4736]{1,0:T(8,128)} async-done(((f32[1536,4736]{1,0:T(8,128)}), f32[192,4736]{1,0:T(8,128)}) %reduce-scatter.3.cloned.1.call-update) | async-done | bytes 3637264 | tf_op jit(solution)/shard_map/reduce_scatter | solution.py:27
  749.8 31.6 %fusion.58 = bf16[1,1536,1536]{2,1,0:T(8,128)(2,1)} fusion(f32[1536,1536]{1,0:T(8,128)} %fusion.42, bf16[1536,1536]{1,0:T(8,128)(2,1)} %copy-done.17, bf16[1536,4480]{1,0:T(8,128)(2,1)} %fusion.17, bf16[1,1536,8960]{2,1,0:T(8,128)(2,1)} %param.14, u32[]{:T(128)S(6)} %mul.230), kind=kOutput, calls=%fused_computation.71 | convolution fusion | flops 21148729344 | bytes 46399492 | tf_op jit(solution)/shard_map/dot_general | solution.py:15
  781.3 6.0 convolution_bitcast_fusion.2
  793.0 4.4 maximum_select_fusion.1
  (123 shorter events, 82.3 us)
Async XLA Ops:
  8.0 475.9 %all-gather.4.cloned.1.call-start = ((), (), s32[]{:S(2)}) async-start(), calls=%async_computation.6 | async-start | bytes 6684672 | tf_op jit(solution)/shard_map/all_gather | solution.py:23
  9.8 64.6 %copy-start.11 = (bf16[1,1536,2,128]{3,2,1,0:T(2,128)(2,1)S(1)}, bf16[1,1536,2,128]{3,2,1,0:T(2,128)(2,1)}, u32[]{:S(2)}) copy-start(bf16[1,1536,2,128]{3,2,1,0:T(2,128)(2,1)} %param.16) | copy-start | bytes 2359300
  9.9 128.8 %collective-permute-start = (bf16[64,3072]{1,0:T(8,128)(2,1)}, bf16[64,3072]{1,0:T(8,128)(2,1)}, u32[]{:S(2)}, u32[]{:S(2)}) collective-permute-start(bf16[64,3072]{1,0:T(8,128)(2,1)} %pad_maximum_fusion.4), channel_id=1, source_target_pairs={{0,4},{2,6},{4,0},{6,2},{1,5},{3,7},{5,1},{7,3},{8,12},{10,14},{12... | collective-permute-start | bytes 1179656 | tf_op jit(solution)/shard_map/ppermute | solution.py:50
  75.5 55.6 %copy-start.12 = (bf16[1,1536,2,128]{3,2,1,0:T(2,128)(2,1)S(1)}, bf16[1,1536,2,128]{3,2,1,0:T(2,128)(2,1)}, u32[]{:S(2)}) copy-start(bf16[1,1536,2,128]{3,2,1,0:T(2,128)(2,1)} %param.17) | copy-start | bytes 2359300
  138.6 7.9 copy-start.6
  153.1 334.5 %all-gather.8.cloned.1.call-start = ((), (), s32[]{:S(2)}) async-start(), calls=%async_computation.8 | async-start | bytes 19496960 | tf_op jit(solution)/shard_map/all_gather | solution.py:23
  183.1 364.7 %all-gather.6.cloned.1.call-start = ((), (), s32[]{:S(2)}) async-start(), calls=%async_computation.7 | async-start | bytes 6684672 | tf_op jit(solution)/shard_map/all_gather | solution.py:23
  183.1 66.6 %collective-permute-start.1 = (bf16[1536,8960]{1,0:T(8,128)(2,1)}, bf16[1536,8960]{1,0:T(8,128)(2,1)}, u32[]{:S(2)}, u32[]{:S(2)}) collective-permute-start(bf16[1536,8960]{1,0:T(8,128)(2,1)} %get-tuple-element.50), channel_id=1, source_target_pairs={{0,1},{1,0},{2,3},{3,2},{4,5},{5,4},{6,7},{7,6},{8,9},{9,8},{10,11... | collective-permute-start | bytes 82575368 | tf_op jit(solution)/shard_map/ppermute | solution.py:65
  183.2 103.9 %collective-permute-start.3 = (bf16[1536,1536]{1,0:T(8,128)(2,1)}, bf16[1536,1536]{1,0:T(8,128)(2,1)}, u32[]{:S(2)}, u32[]{:S(2)}) collective-permute-start(bf16[1536,1536]{1,0:T(8,128)(2,1)} %add_convert_fusion.1), channel_id=1, source_target_pairs={{0,1},{1,0},{2,3},{3,2},{4,5},{5,4},{6,7},{7,6},{8,9},{9,8},{10,11... | collective-permute-start | bytes 14155784 | tf_op jit(solution)/shard_map/ppermute | solution.py:65
  202.9 353.2 %reduce-scatter.5.cloned.1.call-start = ((), (), s32[]{:S(2)}) async-start(), calls=%async_computation.5 | async-start | bytes 30965760 | tf_op jit(solution)/shard_map/reduce_scatter | solution.py:27
  212.7 35.9 %collective-permute-start.2 = (bf16[1536,512]{0,1:T(8,128)(2,1)S(1)}, bf16[1536,512]{0,1:T(8,128)(2,1)S(1)}, u32[]{:S(2)}, u32[]{:S(2)}) collective-permute-start(bf16[1536,512]{0,1:T(8,128)(2,1)S(1)} %pad_maximum_fusion.1), channel_id=1, source_target_pairs={{0,1},{1,0},{2,3},{3,2},{4,5},{5,4},{6,7},{7,6},{8,9},{9,8},{10,11... | collective-permute-start | bytes 4718600 | tf_op jit(solution)/shard_map/ppermute | solution.py:65
  217.7 30.9 %copy-start.17 = (bf16[1536,1536]{1,0:T(8,128)(2,1)}, bf16[1536,1536]{1,0:T(8,128)(2,1)S(1)}, u32[]{:S(2)}) copy-start(bf16[1536,1536]{1,0:T(8,128)(2,1)S(1)} %convolution_convert_fusion.2) | copy-start | bytes 14155780
  287.1 459.8 %reduce-scatter.3.cloned.1.call-start = ((), (), s32[]{:S(2)}) async-start(), calls=%async_computation.4 | async-start | bytes 32735232 | tf_op jit(solution)/shard_map/reduce_scatter | solution.py:27
  287.2 137.0 %collective-permute-start.5 = (bf16[1536,1536]{1,0:T(8,128)(2,1)}, bf16[1536,1536]{1,0:T(8,128)(2,1)}, u32[]{:S(2)}, u32[]{:S(2)}) collective-permute-start(bf16[1536,1536]{1,0:T(8,128)(2,1)} %bitcast.221), channel_id=1, source_target_pairs={{0,1},{1,0},{2,3},{3,2},{4,5},{5,4},{6,7},{7,6},{8,9},{9,8},{10,11... | collective-permute-start | bytes 14155784 | tf_op jit(solution)/shard_map/ppermute | solution.py:65
  340.9 83.2 %collective-permute-start.4 = (bf16[1536,4480]{1,0:T(8,128)(2,1)}, bf16[1536,4480]{1,0:T(8,128)(2,1)}, u32[]{:S(2)}, u32[]{:S(2)}) collective-permute-start(bf16[1536,4480]{1,0:T(8,128)(2,1)} %fusion.17), channel_id=1, source_target_pairs={{0,1},{1,0},{2,3},{3,2},{4,5},{5,4},{6,7},{7,6},{8,9},{9,8},{10,11... | collective-permute-start | bytes 41287688 | tf_op jit(solution)/shard_map/ppermute | solution.py:65
  389.8 30.6 %copy-start.15 = (bf16[1536,512]{0,1:T(8,128)(2,1)S(1)}, bf16[1536,512]{0,1:T(8,128)(2,1)}, u32[]{:S(2)}) copy-start(bf16[1536,512]{0,1:T(8,128)(2,1)} %copy-done.14) | copy-start | bytes 4718596
  389.8 30.6 %copy-start.16 = (f32[1536,256]{1,0:T(8,128)S(1)}, f32[1536,256]{1,0:T(8,128)}, u32[]{:S(2)}) copy-start(f32[1536,256]{1,0:T(8,128)} %fusion.108) | copy-start | bytes 4718596
  487.7 12.1 %copy-start.8 = (bf16[1536,2,2,128]{3,0,2,1:T(8,128)(2,1)S(1)}, bf16[1536,2,2,128]{3,0,2,1:T(8,128)(2,1)}, u32[]{:S(2)}) copy-start(bf16[1536,2,2,128]{3,0,2,1:T(8,128)(2,1)} %copy-done.6) | copy-start | bytes 4718596
  487.7 12.1 %copy-start.4 = (bf16[2,384,1536]{2,1,0:T(8,128)(2,1)S(1)}, bf16[2,384,1536]{2,1,0:T(8,128)(2,1)}, u32[]{:S(2)}) copy-start(bf16[2,384,1536]{2,1,0:T(8,128)(2,1)} %copy-done.3) | copy-start | bytes 7077892
  503.1 41.2 %all-to-all-start = ((bf16[64,16,752]{2,0,1:T(8,128)(2,1)}), bf16[64,16,752]{2,0,1:T(8,128)(2,1)S(1)}, u32[]{:S(2)}, u32[]{:S(2)}) async-start(bf16[64,16,752]{2,0,1:T(8,128)(2,1)} %pad_maximum_fusion.2), calls=%async_computation.2 | async-start | bytes 3145728 | tf_op jit(solution)/shard_map/all_to_all | solution.py:139
  511.5 269.8 %collective-permute-start.6 = (bf16[64,1536]{1,0:T(8,128)(2,1)}, bf16[64,1536]{1,0:T(8,128)(2,1)S(1)}, u32[]{:S(2)}, u32[]{:S(2)}) collective-permute-start(bf16[64,1536]{1,0:T(8,128)(2,1)} %fusion.82), channel_id=1, source_target_pairs={{0,4},{2,6},{4,0},{6,2},{1,5},{3,7},{5,1},{7,3},{8,12},{10,14},{12... | collective-permute-start | bytes 589832 | tf_op jit(solution)/shard_map/ppermute | solution.py:136
  552.7 234.6 %all-to-all-start.1 = ((f32[16,96,192]{1,2,0:T(8,128)}), f32[16,96,192]{1,2,0:T(8,128)S(1)}, u32[]{:S(2)}, u32[]{:S(2)}) async-start(f32[16,96,192]{1,2,0:T(8,128)} %copy.61), calls=%async_computation.3 | async-start | bytes 3145728 | tf_op jit(solution)/shard_map/all_to_all | solution.py:146
  559.6 233.4 %collective-permute-start.8 = (f32[560,768]{1,0:T(8,128)}, f32[560,768]{1,0:T(8,128)}, u32[]{:S(2)}, u32[]{:S(2)}) collective-permute-start(f32[560,768]{1,0:T(8,128)} %get-tuple-element.41), channel_id=1, source_target_pairs={{0,1},{1,0},{2,3},{3,2},{4,5},{5,4},{6,7},{7,6},{8,9},{9,8},{10,11... | collective-permute-start | bytes 5160968 | tf_op jit(solution)/shard_map/ppermute | solution.py:65
  749.8 47.9 %collective-permute-start.7 = (f32[96,4736]{1,0:T(8,128)}, f32[96,4736]{1,0:T(8,128)}, u32[]{:S(2)}, u32[]{:S(2)}) collective-permute-start(f32[96,4736]{1,0:T(8,128)} %constant_dynamic-slice_fusion), channel_id=1, source_target_pairs={{0,1},{1,0},{2,3},{3,2},{4,5},{5,4},{6,7},{7,6},{8,9},{9,8},{10,11... | collective-permute-start | bytes 5455880 | tf_op jit(solution)/shard_map/ppermute | solution.py:65
  (10 other events, 29.0 us)
Sparse Core Ops, SparseCore 0:
  153.2 42.7 all-gather.3
  198.3 81.6 all-gather.7
  282.2 59.2 all-gather.5
Sparse Core Ops, SparseCore 1:
  287.2 213.9 reduce-scatter.4
  505.4 241.5 reduce-scatter.2

commit v3 on v2

--- a/solution.py
+++ b/solution.py
@@ -1,6 +1,8 @@
 import jax
 import jax.numpy as jnp
 from jax import lax
+from jax.experimental import pallas as pl
+from jax.experimental.pallas import tpu as pltpu
 from jax.experimental.layout import Layout, with_layout_constraint
 from jax.sharding import PartitionSpec as P
 
@@ -27,6 +29,40 @@
     return lax.psum_scatter(own, CHIPS, scatter_dimension=0, tiled=True)
 
 
+def dec_mlp_kernel(mid_ref, cot_ref, w1_ref, w2_ref, act_ref, gpre_ref, gmid_ref, acc_ref):
+    @pl.when(pl.program_id(0) == 0)
+    def _():
+        acc_ref[...] = jnp.zeros_like(acc_ref)
+
+    act, gelu_pull = jax.vjp(jax.nn.gelu, dot(mid_ref[...], w1_ref[...], 1, 0))
+    act_ref[...] = act.astype(BF16)
+    g_act = dot(w2_ref[...], cot_ref[...], 1, 1).T.astype(BF16)
+    g_pre = gelu_pull(g_act.astype(F32))[0].astype(BF16)
+    gpre_ref[...] = g_pre
+    acc_ref[...] += dot(w1_ref[...], g_pre, 1, 1)
+
+    @pl.when(pl.program_id(0) == pl.num_programs(0) - 1)
+    def _():
+        gmid_ref[...] = (cot_ref[...].astype(F32) + acc_ref[...].T).astype(BF16)
+
+
+def dec_mlp(mid, cot, w_1, w_2, block):
+    s_dec, d_model = mid.shape
+    width = w_1.shape[1]
+    rows = pl.BlockSpec((s_dec, d_model), lambda i: (0, 0))
+    cols = pl.BlockSpec((s_dec, block), lambda i: (0, i))
+    return pl.pallas_call(
+        dec_mlp_kernel,
+        grid=(width // block,),
+        in_specs=[rows, rows, pl.BlockSpec((d_model, block), lambda i: (0, i)), pl.BlockSpec((block, d_model), lambda i: (i, 0))],
+        out_specs=[cols, cols, rows],
+        out_shape=[jax.ShapeDtypeStruct((s_dec, width), BF16)] * 2 + [jax.ShapeDtypeStruct((s_dec, d_model), BF16)],
+        scratch_shapes=[pltpu.VMEM((d_model, s_dec), F32)],
+        compiler_params=pltpu.CompilerParams(dimension_semantics=('arbitrary',), vmem_limit_bytes=32 * 2 ** 20),
+        cost_estimate=pl.CostEstimate(flops=6 * s_dec * d_model * width, bytes_accessed=4 * d_model * width, transcendentals=s_dec * width),
+    )(mid, cot, w_1, w_2)
+
+
 def solution(mesh):
     n_data, chips = mesh.shape['data'], mesh.shape['stage'] // 2
     n_dev = n_data * chips * 2
@@ -47,9 +83,10 @@
         w_q, w_o, w_1, w_2 = w_query[0], w_out[0], w_ff1[0], w_ff2[0]
         w_kv = jnp.concatenate([w_key[0].reshape(d_model, kv_width), w_val[0].reshape(d_model, kv_width)], axis=1)
 
-        hg = lax.ppermute(jnp.concatenate([h_dec[0], cot_out[0]], axis=1), 'chip', partner_perm)
+        hg_own = jnp.concatenate([h_dec[0], cot_out[0]], axis=1)
+        hg = lax.ppermute(hg_own, 'chip', partner_perm)
         hid, cot = hg[:, :d_model], hg[:, d_model:]
-        hg_all = gather(hg)
+        hg_all = gather(hg_own)
         hid_all, cot_all = hg_all[:, :d_model], hg_all[:, d_model:]
         s_dec = hid.shape[0]
 
@@ -89,12 +126,8 @@
         mid = (hid.astype(F32) + dot(ctx, w_o, 1, 0)).astype(BF16)
         cm_all = gather(jnp.concatenate([ctx, mid], axis=1))
         ctx_all, mid_all = cm_all[:, :d_model], cm_all[:, d_model:]
-        dec_act, dec_pull = jax.vjp(jax.nn.gelu, dot(mid, w_1, 1, 0))
-        dec_act = dec_act.astype(BF16)
-        dec_gact = dot(cot, w_2, 1, 1).astype(BF16)
-        dec_gpre = dec_pull(dec_gact.astype(F32))[0].astype(BF16)
+        dec_act, dec_gpre, g_mid = dec_mlp(mid, cot, w_1, w_2, w_1.shape[1] // 10)
         gpre_all = gather(dec_gpre)
-        g_mid = (cot.astype(F32) + dot(dec_gpre, w_1, 1, 1)).astype(BF16)
         g_ctx = heads_of(dot(g_mid, w_o, 1, 1).astype(BF16))
         g_prob = bdot(g_ctx, val_h, 2, 2)
         g_val = bdot(prob_bf, g_ctx, 1, 1).astype(BF16)
@@ -138,7 +171,10 @@
         sent = [t.reshape(s_dec, n_dev, -1) for t in (dec_act, g_mid, g_query)]
         cols = lax.all_to_all(jnp.concatenate(sent, axis=2), AXES, split_axis=1, concat_axis=0, tiled=True)
         cols = cols.reshape(n_dev * s_dec, -1)
-        act_c, gmid_c, gq_c = cols[:, :n2], cols[:, n2:n2 + n1], cols[:, n2 + n1:]
+        gmid_c = cols[:, n2:n2 + n1]
+        halves = cols.reshape(n_data, 2, chips // 2, 2 * s_dec, -1)
+        cols = jnp.concatenate([halves[:, 1:], halves[:, :1]], axis=1).reshape(n_dev * s_dec, -1)
+        act_c, gq_c = cols[:, :n2], cols[:, n2 + n1:]
         g_w2 = dot(act_c, cot_all, 0, 0)
         mid_c = lax.dynamic_slice_in_dim(mid_all, lax.axis_index(AXES) * n1, n1, 1)
         g_w1 = dot(mid_c, gpre_all, 0, 0)

time: 818 us -> 814 us (level)
  matrix products: 529 us -> 490 us
  Pallas kernels: 0 us -> 37.3 us
    dot_general x25 -> x22, matrix products: 513 us -> 471 us  [dot(): lax.dot_general(lhs, rhs, (((lhs_dim,), (rhs_dim,)), ((), ())), preferred...]
    pallas_call x0 -> x1, Pallas kernels: none -> 37.3 us  [dec_mlp(): pl.pallas_call(dec_mlp_kernel, grid=(width // block,), in_specs=[rows, ro...]
  transfers between devices with their start and end apart: 16 -> 16, of which waited for: 1 -> 1; matrix products, arithmetic and copies ran while one was open for 70% -> 66% of each run, Pallas kernels for 0% -> 5%
where the time goes in v3:
time: 814 us; the launch traced here: 808 us
  matrix products  490 us (60%)
  waiting for transfers between devices  184 us (23%)
  Pallas kernels  37.3 us (5%)
  local copies, waits for them, and re-layouts  34.7 us (4%)
  other arithmetic  32.4 us (4%)
  between operations  16 us (2%)
  starting transfers between devices  13.7 us (2%)
    dot_general x22, matrix products, dot(): lax.dot_general(lhs, rhs, (((lhs_dim,), (rhs_dim,)), ((), ())), preferred...  471 us
    reduce_scatter x2, waiting for transfers between devices, scatter(): return lax.psum_scatter(own, CHIPS, scatter_dimension=0, tiled=True)  183 us
    pallas_call x1, Pallas kernels, dec_mlp(): pl.pallas_call(dec_mlp_kernel, grid=(width // block,), in_specs=[rows, ro...  37.3 us
    concatenate x1, other arithmetic, step(): jnp.concatenate([up_half, wkv_half], axis=1)  20.4 us
  transfers between devices with their start and end apart: 16, of which 1 were waited for; matrix products, arithmetic and copies ran while one was open for 66% of the time, Pallas kernels for 5%

profile of v3, /device:TPU:0, one launch (start us, length us, event | category | flops | bytes accessed | tf_op | source)
XLA Modules:
  0.0 808.2 jit_solution(5152923194362642905)
XLA Ops:
  13.1 61.4 %fusion.9 = (bf16[1536,8960]{1,0:T(8,128)(2,1)}, f32[1536,8960]{1,0:T(8,128)}) fusion(bf16[1,1536,8960]{2,1,0:T(8,128)(2,1)} %param.14, bf16[1,1536,1536]{2,1,0:T(8,128)(2,1)} %param.11), kind=kOutput, calls=%fused_computation.10 | convolution fusion | flops 42402447360 | bytes 114819072 | tf_op jit(solution)/shard_map/dot_general | solution.py:17
  74.6 55.6 %add_convert_fusion.1 = bf16[1536,1536]{1,0:T(8,128)(2,1)} fusion(bf16[1536,8960]{1,0:T(8,128)(2,1)} %get-tuple-element.58, bf16[1,8960,1536]{2,1,0:T(8,128)(2,1)} %param.15, bf16[1,1536,1536]{2,1,0:T(8,128)(2,1)} %param.11), kind=kOutput, calls=%fused_computation.61 | convolution fusion | flops 42285662208 | bytes 64487424 | tf_op jit(solution)/shard_map/dot_general | solution.py:17
  130.4 6.7 convolution_convert_fusion.4
  139.3 3.9 fusion.73
  154.8 37.3 %shard_map.186 = (bf16[64,8960]{1,0:T(8,128)(2,1)S(1)}, bf16[64,8960]{1,0:T(8,128)(2,1)}, bf16[64,1536]{1,0:T(8,128)(2,1)S(1)}) custom-call(bf16[64,1536]{1,0:T(8,128)(2,1)S(1)} %add_convert_fusion.2.mid_ref, bf16[64,1536]{1,0:T(8,128)(2,1)S(1)} %slice.103.cot_ref, bf16[1536,8960]{1,0:T(8,128)(2,1)} %bitcast.178, bf16[8960,1536]{1,0:T(8,128)(2,1)} %bitcast.179), custom_call_target="tpu_custom_call" | custom-call | flops 5284823040 | bytes 55050240 | tf_op jit(solution)/shard_map/pallas_call | solution.py:54
  193.5 4.0 fusion.76
  197.9 4.0 convolution_convert_fusion.5
  201.9 6.7 multiply_convert_fusion
  215.1 32.1 %fusion.64 = f32[8960,768]{1,0:T(8,128)} fusion(bf16[1536,8960]{1,0:T(8,128)(2,1)} %get-tuple-element.58, bf16[1536,1536]{1,0:T(8,128)(2,1)S(1)} %convolution_convert_fusion.2, u32[]{:T(128)S(6)} %mul.157), kind=kOutput, calls=%fused_computation.91 | convolution fusion | flops 21139292160 | bytes 57409540 | tf_op jit(solution)/shard_map/dot_general | solution.py:17
  248.3 37.1 %convolution_add_fusion = f32[8960,768]{1,0:T(8,128)} fusion(f32[8960,768]{1,0:T(8,128)} %fusion.64, bf16[1536,8960]{1,0:T(8,128)(2,1)} %collective-permute-done.1, bf16[1536,512]{0,1:T(8,128)(2,1)} %copy-done.18, bf16[1536,512]{1,0:T(8,128)(2,1)S(1)} %copy-done.16, u32[]{:T(128)S(6)} %mul.157), kind=kOutput, calls=%fused_computation.48 | convolution fusion | flops 22355312640 | bytes 84934656 | tf_op jit(solution)/shard_map/dot_general | solution.py:17
  286.8 5.1 fusion.87
  291.9 47.1 %fusion.17 = bf16[1536,4480]{1,0:T(8,128)(2,1)} fusion(f32[1536,8960]{1,0:T(8,128)} %get-tuple-element.59, u32[]{:T(128)S(6)} %mul.172, bf16[1536,1536]{1,0:T(8,128)(2,1)} %copy-done.21, bf16[1,8960,1536]{2,1,0:T(8,128)(2,1)} %param.15), kind=kOutput, calls=%fused_computation.27 | convolution fusion | flops 21290680320 | bytes 59769856 | tf_op jit(solution)/shard_map/dot_general | solution.py:17
  339.4 47.3 %fusion.12 = bf16[1536,4480]{1,0:T(8,128)(2,1)} fusion(f32[1536,8960]{1,0:T(8,128)} %get-tuple-element.59, u32[]{:T(128)S(6)} %mul.158, bf16[1536,1536]{1,0:T(8,128)(2,1)} %copy-done.21, bf16[1,8960,1536]{2,1,0:T(8,128)(2,1)} %param.15), kind=kOutput, calls=%fused_computation.22 | convolution fusion | flops 21290680320 | bytes 59769856 | tf_op jit(solution)/shard_map/dot_general | solution.py:17
  386.7 31.3 %convolution_bitcast_fusion = f32[1536,4480]{1,0:T(8,128)} fusion(bf16[1536,4480]{1,0:T(8,128)(2,1)} %fusion.12, bf16[1,1536,1536]{2,1,0:T(8,128)(2,1)} %param.11), kind=kOutput, calls=%fused_computation.45 | convolution fusion | flops 21139292160 | bytes 46006272 | tf_op jit(solution)/shard_map/dot_general | solution.py:17
  421.9 36.1 %bitcast_add_fusion = f32[1536,4480]{1,0:T(8,128)} fusion(f32[1536,4480]{1,0:T(8,128)} %convolution_bitcast_fusion, bf16[1536,4480]{1,0:T(8,128)(2,1)} %collective-permute-done.4, bf16[1536,1536]{1,0:T(8,128)(2,1)} %collective-permute-done.5), kind=kOutput, calls=%fused_computation.40 | convolution fusion | flops 21146173440 | bytes 73531392 | tf_op jit(solution)/shard_map/dot_general | solution.py:17
  458.0 20.4 %pad_maximum_fusion = f32[1536,4736]{1,0:T(8,128)} fusion(f32[1536,256]{1,0:T(8,128)S(1)} %convolution_add_fusion.1, f32[1536,4480]{1,0:T(8,128)} %bitcast_add_fusion), kind=kLoop, calls=%fused_computation.19 | loop fusion | flops 7274496 | bytes 58195968 | tf_op jit(solution)/shard_map/concatenate | solution.py:156
  484.3 12.4 %convolution_bitcast_fusion.1 = f32[1,96,8960]{2,1,0:T(8,128)} fusion(bf16[1024,8960]{1,0:T(8,128)(2,1)} %all-gather.8.cloned.1.call-done, bf16[1024,1536]{1,0:T(8,128)(2,1)} %slice.120, s32[]{:T(128)S(6)} %select_n.47), kind=kOutput, calls=%fused_computation.59 | convolution fusion | flops 1761607680 | bytes 22052868 | tf_op jit(solution)/shard_map/dot_general | solution.py:17
  502.9 4.5 fusion.70
  509.4 31.9 %fusion.36 = f32[1536,1536]{1,0:T(8,128)} fusion(bf16[1536,4480]{1,0:T(8,128)(2,1)} %fusion.12, bf16[1,1536,8960]{2,1,0:T(8,128)(2,1)} %param.14, u32[]{:T(128)S(6)} %mul.158), kind=kOutput, calls=%fused_computation.51 | convolution fusion | flops 21139292160 | bytes 36962308 | tf_op jit(solution)/shard_map/dot_general | solution.py:17
  541.6 4.2 fusion.62
  559.9 183.4 %reduce-scatter.3.cloned.1.call-done = f32[192,4736]{1,0:T(8,128)} async-done(((f32[1536,4736]{1,0:T(8,128)}), f32[192,4736]{1,0:T(8,128)}) %reduce-scatter.3.cloned.1.call-update) | async-done | bytes 3637264 | tf_op jit(solution)/shard_map/reduce_scatter | solution.py:29
  746.2 31.5 %fusion.46 = bf16[1,1536,1536]{2,1,0:T(8,128)(2,1)} fusion(f32[1536,1536]{1,0:T(8,128)} %fusion.36, bf16[1536,1536]{1,0:T(8,128)(2,1)} %copy-done.21, bf16[1536,4480]{1,0:T(8,128)(2,1)} %fusion.17, bf16[1,1536,8960]{2,1,0:T(8,128)(2,1)} %param.14, u32[]{:T(128)S(6)} %mul.172), kind=kOutput, calls=%fused_computation.63 | convolution fusion | flops 21148729344 | bytes 46399492 | tf_op jit(solution)/shard_map/dot_general | solution.py:17
  777.7 6.0 convolution_bitcast_fusion.2
  789.4 4.4 maximum_select_fusion.1
  (132 shorter events, 77.6 us)
Async XLA Ops:
  8.0 472.6 %all-gather.4.cloned.1.call-start = ((), (), s32[]{:S(2)}) async-start(), calls=%async_computation.6 | async-start | bytes 6684672 | tf_op jit(solution)/shard_map/all_gather | solution.py:25
  9.9 64.6 %copy-start.11 = (bf16[1,1536,2,128]{3,2,1,0:T(2,128)(2,1)S(1)}, bf16[1,1536,2,128]{3,2,1,0:T(2,128)(2,1)}, u32[]{:S(2)}) copy-start(bf16[1,1536,2,128]{3,2,1,0:T(2,128)(2,1)} %param.16) | copy-start | bytes 2359300
  9.9 129.5 %collective-permute-start = (bf16[64,3072]{1,0:T(8,128)(2,1)}, bf16[64,3072]{1,0:T(8,128)(2,1)}, u32[]{:S(2)}, u32[]{:S(2)}) collective-permute-start(bf16[64,3072]{1,0:T(8,128)(2,1)} %pad_maximum_fusion.5), channel_id=1, source_target_pairs={{0,4},{2,6},{4,0},{6,2},{1,5},{3,7},{5,1},{7,3},{8,12},{10,14},{12... | collective-permute-start | bytes 1179656 | tf_op jit(solution)/shard_map/ppermute | solution.py:87
  74.6 55.7 %copy-start.12 = (bf16[1,1536,2,128]{3,2,1,0:T(2,128)(2,1)S(1)}, bf16[1,1536,2,128]{3,2,1,0:T(2,128)(2,1)}, u32[]{:S(2)}) copy-start(bf16[1,1536,2,128]{3,2,1,0:T(2,128)(2,1)} %param.17) | copy-start | bytes 2359300
  139.3 58.5 %copy-start.6 = (bf16[1536,2,2,128]{3,0,2,1:T(8,128)(2,1)}, bf16[1536,2,2,128]{3,0,2,1:T(8,128)(2,1)S(1)}, u32[]{:S(2)}) copy-start(bf16[1536,2,2,128]{3,0,2,1:T(8,128)(2,1)S(1)} %copy.49) | copy-start | bytes 4718596
  153.8 330.5 %all-gather.8.cloned.1.call-start = ((), (), s32[]{:S(2)}) async-start(), calls=%async_computation.8 | async-start | bytes 19496960 | tf_op jit(solution)/shard_map/all_gather | solution.py:25
  192.1 353.7 %all-gather.6.cloned.1.call-start = ((), (), s32[]{:S(2)}) async-start(), calls=%async_computation.7 | async-start | bytes 6684672 | tf_op jit(solution)/shard_map/all_gather | solution.py:25
  192.2 56.1 %collective-permute-start.1 = (bf16[1536,8960]{1,0:T(8,128)(2,1)}, bf16[1536,8960]{1,0:T(8,128)(2,1)}, u32[]{:S(2)}, u32[]{:S(2)}) collective-permute-start(bf16[1536,8960]{1,0:T(8,128)(2,1)} %get-tuple-element.58), channel_id=1, source_target_pairs={{0,1},{1,0},{2,3},{3,2},{4,5},{5,4},{6,7},{7,6},{8,9},{9,8},{10,11... | collective-permute-start | bytes 82575368 | tf_op jit(solution)/shard_map/ppermute | solution.py:102
  192.2 93.2 %collective-permute-start.3 = (bf16[1536,1536]{1,0:T(8,128)(2,1)}, bf16[1536,1536]{1,0:T(8,128)(2,1)}, u32[]{:S(2)}, u32[]{:S(2)}) collective-permute-start(bf16[1536,1536]{1,0:T(8,128)(2,1)} %add_convert_fusion.1), channel_id=1, source_target_pairs={{0,1},{1,0},{2,3},{3,2},{4,5},{5,4},{6,7},{7,6},{8,9},{9,8},{10,11... | collective-permute-start | bytes 14155784 | tf_op jit(solution)/shard_map/ppermute | solution.py:102
  192.9 363.1 %reduce-scatter.5.cloned.1.call-start = ((), (), s32[]{:S(2)}) async-start(), calls=%async_computation.5 | async-start | bytes 30965760 | tf_op jit(solution)/shard_map/reduce_scatter | solution.py:29
  211.9 35.3 %collective-permute-start.2 = (bf16[1536,512]{0,1:T(8,128)(2,1)S(1)}, bf16[1536,512]{0,1:T(8,128)(2,1)S(1)}, u32[]{:S(2)}, u32[]{:S(2)}) collective-permute-start(bf16[1536,512]{0,1:T(8,128)(2,1)S(1)} %pad_maximum_fusion.1), channel_id=1, source_target_pairs={{0,1},{1,0},{2,3},{3,2},{4,5},{5,4},{6,7},{7,6},{8,9},{9,8},{10,11... | collective-permute-start | bytes 4718600 | tf_op jit(solution)/shard_map/ppermute | solution.py:102
  215.1 32.1 %copy-start.21 = (bf16[1536,1536]{1,0:T(8,128)(2,1)}, bf16[1536,1536]{1,0:T(8,128)(2,1)S(1)}, u32[]{:S(2)}) copy-start(bf16[1536,1536]{1,0:T(8,128)(2,1)S(1)} %convolution_convert_fusion.2) | copy-start | bytes 14155780
  215.1 33.2 %copy-start.16 = (bf16[1536,512]{1,0:T(8,128)(2,1)S(1)}, bf16[1536,512]{1,0:T(8,128)(2,1)}, u32[]{:S(2)}) copy-start(bf16[1536,512]{1,0:T(8,128)(2,1)} %copy-done.14) | copy-start | bytes 4718596
  285.4 457.9 %reduce-scatter.3.cloned.1.call-start = ((), (), s32[]{:S(2)}) async-start(), calls=%async_computation.4 | async-start | bytes 32735232 | tf_op jit(solution)/shard_map/reduce_scatter | solution.py:29
  285.5 136.4 %collective-permute-start.5 = (bf16[1536,1536]{1,0:T(8,128)(2,1)}, bf16[1536,1536]{1,0:T(8,128)(2,1)}, u32[]{:S(2)}, u32[]{:S(2)}) collective-permute-start(bf16[1536,1536]{1,0:T(8,128)(2,1)} %bitcast.210), channel_id=1, source_target_pairs={{0,1},{1,0},{2,3},{3,2},{4,5},{5,4},{6,7},{7,6},{8,9},{9,8},{10,11... | collective-permute-start | bytes 14155784 | tf_op jit(solution)/shard_map/ppermute | solution.py:102
  339.0 82.9 %collective-permute-start.4 = (bf16[1536,4480]{1,0:T(8,128)(2,1)}, bf16[1536,4480]{1,0:T(8,128)(2,1)}, u32[]{:S(2)}, u32[]{:S(2)}) collective-permute-start(bf16[1536,4480]{1,0:T(8,128)(2,1)} %fusion.17), channel_id=1, source_target_pairs={{0,1},{1,0},{2,3},{3,2},{4,5},{5,4},{6,7},{7,6},{8,9},{9,8},{10,11... | collective-permute-start | bytes 41287688 | tf_op jit(solution)/shard_map/ppermute | solution.py:102
  386.7 31.3 %copy-start.19 = (bf16[1536,512]{0,1:T(8,128)(2,1)S(1)}, bf16[1536,512]{0,1:T(8,128)(2,1)}, u32[]{:S(2)}) copy-start(bf16[1536,512]{0,1:T(8,128)(2,1)} %copy-done.18) | copy-start | bytes 4718596
  386.7 31.3 %copy-start.20 = (f32[1536,256]{1,0:T(8,128)S(1)}, f32[1536,256]{1,0:T(8,128)}, u32[]{:S(2)}) copy-start(f32[1536,256]{1,0:T(8,128)} %fusion.87) | copy-start | bytes 4718596
  484.3 12.4 %copy-start.7 = (bf16[1536,2,2,128]{3,0,2,1:T(8,128)(2,1)S(1)}, bf16[1536,2,2,128]{3,0,2,1:T(8,128)(2,1)}, u32[]{:S(2)}) copy-start(bf16[1536,2,2,128]{3,0,2,1:T(8,128)(2,1)} %copy-done.6) | copy-start | bytes 4718596
  500.1 41.3 %all-to-all-start = ((bf16[64,16,752]{2,0,1:T(8,128)(2,1)}), bf16[64,16,752]{2,0,1:T(8,128)(2,1)S(1)}, u32[]{:S(2)}, u32[]{:S(2)}) async-start(bf16[64,16,752]{2,0,1:T(8,128)(2,1)} %pad_maximum_fusion.2), calls=%async_computation.2 | async-start | bytes 3145728 | tf_op jit(solution)/shard_map/all_to_all | solution.py:172
  507.4 270.3 %collective-permute-start.6 = (bf16[64,1536]{1,0:T(8,128)(2,1)}, bf16[64,1536]{1,0:T(8,128)(2,1)S(1)}, u32[]{:S(2)}, u32[]{:S(2)}) collective-permute-start(bf16[64,1536]{1,0:T(8,128)(2,1)} %fusion.70), channel_id=1, source_target_pairs={{0,4},{2,6},{4,0},{6,2},{1,5},{3,7},{5,1},{7,3},{8,12},{10,14},{12... | collective-permute-start | bytes 589832 | tf_op jit(solution)/shard_map/ppermute | solution.py:169
  553.1 230.7 %all-to-all-start.1 = ((f32[16,96,192]{1,2,0:T(8,128)}), f32[16,96,192]{1,2,0:T(8,128)S(1)}, u32[]{:S(2)}, u32[]{:S(2)}) async-start(f32[16,96,192]{1,2,0:T(8,128)} %copy.61), calls=%async_computation.3 | async-start | bytes 3145728 | tf_op jit(solution)/shard_map/all_to_all | solution.py:182
  559.4 230.0 %collective-permute-start.8 = (f32[560,768]{1,0:T(8,128)}, f32[560,768]{1,0:T(8,128)}, u32[]{:S(2)}, u32[]{:S(2)}) collective-permute-start(f32[560,768]{1,0:T(8,128)} %get-tuple-element.47), channel_id=1, source_target_pairs={{0,1},{1,0},{2,3},{3,2},{4,5},{5,4},{6,7},{7,6},{8,9},{9,8},{10,11... | collective-permute-start | bytes 5160968 | tf_op jit(solution)/shard_map/ppermute | solution.py:102
  746.2 47.9 %collective-permute-start.7 = (f32[96,4736]{1,0:T(8,128)}, f32[96,4736]{1,0:T(8,128)}, u32[]{:S(2)}, u32[]{:S(2)}) collective-permute-start(f32[96,4736]{1,0:T(8,128)} %constant_dynamic-slice_fusion), channel_id=1, source_target_pairs={{0,1},{1,0},{2,3},{3,2},{4,5},{5,4},{6,7},{7,6},{8,9},{9,8},{10,11... | collective-permute-start | bytes 5455880 | tf_op jit(solution)/shard_map/ppermute | solution.py:102
  (14 other events, 66.5 us)
Sparse Core Ops, SparseCore 0:
  153.9 42.7 all-gather.3
  199.0 81.5 all-gather.7
  283.4 61.2 all-gather.5
Sparse Core Ops, SparseCore 1:
  285.5 215.1 reduce-scatter.4
  504.9 238.4 reduce-scatter.2

commit v4 on v3

--- a/solution.py
+++ b/solution.py
@@ -1,3 +1,5 @@
+import functools
+
 import jax
 import jax.numpy as jnp
 from jax import lax
@@ -63,6 +65,43 @@
     )(mid, cot, w_1, w_2)
 
 
+def enc_mlp_kernel(rows, x_ref, up_ref, down_ref, pre_ref, act_ref, mem_ref, acc_ref):
+    step = pl.program_id(0)
+
+    @pl.when(step == 0)
+    def _():
+        acc_ref[...] = jnp.zeros_like(acc_ref)
+
+    @pl.loop(0, x_ref.shape[0] // rows)
+    def _(i):
+        part = pl.ds(pl.multiple_of(i * rows, rows), rows)
+        pre = dot(x_ref[part, :], up_ref[...], 1, 0)
+        pre_ref[part, :] = pre
+        act_ref[part, :] = jax.nn.gelu(pre).astype(BF16)
+        acc_ref[part, :] += dot(act_ref[part, :], down_ref[...], 1, 0)
+
+    @pl.when(step == pl.num_programs(0) - 1)
+    def _():
+        mem_ref[...] = (x_ref[...].astype(F32) + acc_ref[...]).astype(BF16)
+
+
+def enc_mlp(x, up, down, block, rows):
+    seq, d_model = x.shape
+    width = up.shape[1]
+    full = pl.BlockSpec((seq, d_model), lambda i: (0, 0), pipeline_mode=pl.Buffered(1))
+    cols = pl.BlockSpec((seq, block), lambda i: (0, i))
+    return pl.pallas_call(
+        functools.partial(enc_mlp_kernel, rows),
+        grid=(width // block,),
+        in_specs=[full, pl.BlockSpec((d_model, block), lambda i: (0, i)), pl.BlockSpec((block, d_model), lambda i: (i, 0))],
+        out_specs=[cols, cols, full],
+        out_shape=[jax.ShapeDtypeStruct((seq, width), F32), jax.ShapeDtypeStruct((seq, width), BF16), jax.ShapeDtypeStruct((seq, d_model), BF16)],
+        scratch_shapes=[pltpu.VMEM((seq, d_model), F32)],
+        compiler_params=pltpu.CompilerParams(dimension_semantics=('arbitrary',), vmem_limit_bytes=63 * 2 ** 20),
+        cost_estimate=pl.CostEstimate(flops=4 * seq * d_model * width, bytes_accessed=4 * d_model * width + 6 * seq * width, transcendentals=seq * width),
+    )(x, up, down)
+
+
 def solution(mesh):
     n_data, chips = mesh.shape['data'], mesh.shape['stage'] // 2
     n_dev = n_data * chips * 2
@@ -109,10 +148,8 @@
             return jnp.where(core == 0, jnp.concatenate([own, other], axis=1), jnp.concatenate([other, own], axis=1))
 
         x_sib = swap(x)
-        pre = dot(x, up, 1, 0)
-        act = lax.optimization_barrier(jax.nn.gelu(pre).astype(BF16))
+        pre, act, memory = enc_mlp(x, up, down, up.shape[1] // 7, x.shape[0] // 3)
         act_sib = swap(act)
-        memory = (x.astype(F32) + dot(act, down, 1, 0)).astype(BF16)
         mem_sib = swap(memory)
         kv = dot(memory, w_kv, 1, 0).astype(BF16)
         kv_h = kv.reshape(-1, 2, kv_heads, head).transpose(1, 2, 0, 3)
@@ -126,7 +163,7 @@
         mid = (hid.astype(F32) + dot(ctx, w_o, 1, 0)).astype(BF16)
         cm_all = gather(jnp.concatenate([ctx, mid], axis=1))
         ctx_all, mid_all = cm_all[:, :d_model], cm_all[:, d_model:]
-        dec_act, dec_gpre, g_mid = dec_mlp(mid, cot, w_1, w_2, w_1.shape[1] // 10)
+        dec_act, dec_gpre, g_mid = dec_mlp(mid, cot, w_1, w_2, w_1.shape[1] // 7)
         gpre_all = gather(dec_gpre)
         g_ctx = heads_of(dot(g_mid, w_o, 1, 1).astype(BF16))
         g_prob = bdot(g_ctx, val_h, 2, 2)

time: 814 us -> 821 us (level)
  Pallas kernels: 37.3 us -> 156 us
  matrix products: 490 us -> 374 us
    pallas_call x0 -> x1, Pallas kernels: none -> 119 us  [enc_mlp(): pl.pallas_call(functools.partial(enc_mlp_kernel, rows), grid=(width // bl...]
    dot_general x22 -> x20, matrix products: 471 us -> 355 us  [dot(): lax.dot_general(lhs, rhs, (((lhs_dim,), (rhs_dim,)), ((), ())), preferred...]
  transfers between devices with their start and end apart: 16 -> 16, of which waited for: 1 -> 1; matrix products, arithmetic and copies ran while one was open for 66% -> 52% of each run, Pallas kernels for 5% -> 19%
where the time goes in v4:
time: 821 us; the launch traced here: 814 us
  matrix products  374 us (46%)
  waiting for transfers between devices  184 us (22%)
  Pallas kernels  156 us (19%)
  local copies, waits for them, and re-layouts  38.5 us (5%)
  other arithmetic  31.8 us (4%)
  between operations  15.9 us (2%)
  starting transfers between devices  14.1 us (2%)
    dot_general x20, matrix products, dot(): lax.dot_general(lhs, rhs, (((lhs_dim,), (rhs_dim,)), ((), ())), preferred...  355 us
    reduce_scatter x2, waiting for transfers between devices, scatter(): return lax.psum_scatter(own, CHIPS, scatter_dimension=0, tiled=True)  183 us
    pallas_call x1, Pallas kernels, enc_mlp(): pl.pallas_call(functools.partial(enc_mlp_kernel, rows), grid=(width // bl...  119 us
    pallas_call x1, Pallas kernels, dec_mlp(): pl.pallas_call(dec_mlp_kernel, grid=(width // block,), in_specs=[rows, ro...  36.8 us
    concatenate x1, other arithmetic, step(): jnp.concatenate([up_half, wkv_half], axis=1)  20.5 us
  transfers between devices with their start and end apart: 16, of which 1 were waited for; matrix products, arithmetic and copies ran while one was open for 52% of the time, Pallas kernels for 19%

profile of v4, /device:TPU:0, one launch (start us, length us, event | category | flops | bytes accessed | tf_op | source)
XLA Modules:
  0.0 813.9 jit_solution(3519784988003239273)
XLA Ops:
  16.6 119.2 %shard_map.186 = (f32[1536,8960]{1,0:T(8,128)}, bf16[1536,8960]{1,0:T(8,128)(2,1)}, bf16[1536,1536]{1,0:T(8,128)(2,1)}) custom-call(bf16[1536,1536]{1,0:T(8,128)(2,1)} %bitcast.198, bf16[1536,8960]{1,0:T(8,128)(2,1)} %bitcast.197, bf16[8960,1536]{1,0:T(8,128)(2,1)} %bitcast.196), custom_call_target="tpu_custom_call" | custom-call | flops 84557168640 | bytes 137625600 | tf_op jit(solution)/shard_map/pallas_call | solution.py:93
  135.9 6.6 convolution_convert_fusion.4
  144.7 3.9 fusion.59
  160.2 36.8 %shard_map.187 = (bf16[64,8960]{1,0:T(8,128)(2,1)S(1)}, bf16[64,8960]{1,0:T(8,128)(2,1)}, bf16[64,1536]{1,0:T(8,128)(2,1)S(1)}) custom-call(bf16[64,1536]{1,0:T(8,128)(2,1)S(1)} %add_convert_fusion.1.mid_ref, bf16[64,1536]{1,0:T(8,128)(2,1)S(1)} %slice.103.cot_ref, bf16[1536,8960]{1,0:T(8,128)(2,1)} %bitcast.164, bf16[8960,1536]{1,0:T(8,128)(2,1)} %bitcast.165), custom_call_target="tpu_custom_call" | custom-call | flops 5284823040 | bytes 55050240 | tf_op jit(solution)/shard_map/pallas_call | solution.py:56
  198.3 3.9 fusion.62
  202.5 4.0 convolution_convert_fusion.5
  206.6 6.5 multiply_convert_fusion
  216.3 4.8 convolution_convert_fusion.2
  221.1 31.4 %fusion.50 = f32[8960,768]{1,0:T(8,128)} fusion(bf16[1536,8960]{1,0:T(8,128)(2,1)} %get-tuple-element.26, bf16[1536,1536]{1,0:T(8,128)(2,1)S(1)} %convolution_convert_fusion.2, u32[]{:T(128)S(6)} %mul.129), kind=kOutput, calls=%fused_computation.77 | convolution fusion | flops 21139292160 | bytes 57409540 | tf_op jit(solution)/shard_map/dot_general | solution.py:19
  253.7 37.2 %convolution_add_fusion = f32[8960,768]{1,0:T(8,128)} fusion(f32[8960,768]{1,0:T(8,128)} %fusion.50, bf16[1536,8960]{1,0:T(8,128)(2,1)} %collective-permute-done.1, bf16[1536,512]{0,1:T(8,128)(2,1)} %copy-done.14, bf16[1536,512]{1,0:T(8,128)(2,1)} %bitcast_dynamic-update-slice_fusion, u32[]{:T(128)S(6)} %mul.129), kind=kOutput, calls=%fused_computation.35 | convolution fusion | flops 22355312640 | bytes 84934656 | tf_op jit(solution)/shard_map/dot_general | solution.py:19
  292.4 5.1 fusion.73
  297.4 47.0 %fusion.9 = bf16[1536,4480]{1,0:T(8,128)(2,1)} fusion(f32[1536,8960]{1,0:T(8,128)} %get-tuple-element.31, u32[]{:T(128)S(6)} %mul.144, bf16[1536,1536]{1,0:T(8,128)(2,1)} %copy-done.17, bf16[1,8960,1536]{2,1,0:T(8,128)(2,1)} %param.15), kind=kOutput, calls=%fused_computation.18 | convolution fusion | flops 21290680320 | bytes 59769856 | tf_op jit(solution)/shard_map/dot_general | solution.py:19
  345.2 47.3 %fusion.4 = bf16[1536,4480]{1,0:T(8,128)(2,1)} fusion(f32[1536,8960]{1,0:T(8,128)} %get-tuple-element.31, u32[]{:T(128)S(6)} %mul.130, bf16[1536,1536]{1,0:T(8,128)(2,1)} %copy-done.17, bf16[1,8960,1536]{2,1,0:T(8,128)(2,1)} %param.15), kind=kOutput, calls=%fused_computation.13 | convolution fusion | flops 21290680320 | bytes 59769856 | tf_op jit(solution)/shard_map/dot_general | solution.py:19
  392.5 31.5 %convolution_bitcast_fusion = f32[1536,4480]{1,0:T(8,128)} fusion(bf16[1536,4480]{1,0:T(8,128)(2,1)} %fusion.4, bf16[1,1536,1536]{2,1,0:T(8,128)(2,1)} %param.11), kind=kOutput, calls=%fused_computation.32 | convolution fusion | flops 21139292160 | bytes 46006272 | tf_op jit(solution)/shard_map/dot_general | solution.py:19
  427.9 35.7 %bitcast_add_fusion = f32[1536,4480]{1,0:T(8,128)} fusion(f32[1536,4480]{1,0:T(8,128)} %convolution_bitcast_fusion, bf16[1536,4480]{1,0:T(8,128)(2,1)} %collective-permute-done.4, bf16[1536,1536]{1,0:T(8,128)(2,1)} %collective-permute-done.5), kind=kOutput, calls=%fused_computation.31 | convolution fusion | flops 21146173440 | bytes 73531392 | tf_op jit(solution)/shard_map/dot_general | solution.py:19
  463.6 20.5 %pad_maximum_fusion = f32[1536,4736]{1,0:T(8,128)} fusion(f32[1536,256]{1,0:T(8,128)S(1)} %convolution_add_fusion.1, f32[1536,4480]{1,0:T(8,128)} %bitcast_add_fusion), kind=kLoop, calls=%fused_computation.10 | loop fusion | flops 7274496 | bytes 58195968 | tf_op jit(solution)/shard_map/concatenate | solution.py:193
  490.2 12.4 %convolution_bitcast_fusion.1 = f32[1,96,8960]{2,1,0:T(8,128)} fusion(bf16[1024,8960]{1,0:T(8,128)(2,1)} %all-gather.8.cloned.1.call-done, bf16[1024,1536]{1,0:T(8,128)(2,1)} %slice.120, s32[]{:T(128)S(6)} %select_n.47), kind=kOutput, calls=%fused_computation.46 | convolution fusion | flops 1761607680 | bytes 22052868 | tf_op jit(solution)/shard_map/dot_general | solution.py:19
  508.5 4.5 fusion.56
  515.0 31.7 %fusion.24 = f32[1536,1536]{1,0:T(8,128)} fusion(bf16[1536,4480]{1,0:T(8,128)(2,1)} %fusion.4, bf16[1,1536,8960]{2,1,0:T(8,128)(2,1)} %param.14, u32[]{:T(128)S(6)} %mul.130), kind=kOutput, calls=%fused_computation.38 | convolution fusion | flops 21139292160 | bytes 36962308 | tf_op jit(solution)/shard_map/dot_general | solution.py:19
  547.0 4.2 fusion.48
  565.5 183.5 %reduce-scatter.3.cloned.1.call-done = f32[192,4736]{1,0:T(8,128)} async-done(((f32[1536,4736]{1,0:T(8,128)}), f32[192,4736]{1,0:T(8,128)}) %reduce-scatter.3.cloned.1.call-update) | async-done | bytes 3637264 | tf_op jit(solution)/shard_map/reduce_scatter | solution.py:31
  751.8 31.6 %fusion.32 = bf16[1,1536,1536]{2,1,0:T(8,128)(2,1)} fusion(f32[1536,1536]{1,0:T(8,128)} %fusion.24, bf16[1536,1536]{1,0:T(8,128)(2,1)} %copy-done.17, bf16[1536,4480]{1,0:T(8,128)(2,1)} %fusion.9, bf16[1,1536,8960]{2,1,0:T(8,128)(2,1)} %param.14, u32[]{:T(128)S(6)} %mul.144), kind=kOutput, calls=%fused_computation.49 | convolution fusion | flops 21148729344 | bytes 46399492 | tf_op jit(solution)/shard_map/dot_general | solution.py:19
  783.4 6.0 convolution_bitcast_fusion.2
  795.1 4.4 maximum_select_fusion.1
  (123 shorter events, 77.9 us)
Async XLA Ops:
  8.0 478.3 %all-gather.4.cloned.1.call-start = ((), (), s32[]{:S(2)}) async-start(), calls=%async_computation.6 | async-start | bytes 6684672 | tf_op jit(solution)/shard_map/all_gather | solution.py:27
  9.1 126.8 %copy-start.10 = (bf16[64,3072]{1,0:T(8,128)(2,1)}, bf16[64,3072]{1,0:T(8,128)(2,1)S(1)}, u32[]{:S(2)}) copy-start(bf16[64,3072]{1,0:T(8,128)(2,1)S(1)} %pad_maximum_fusion.5) | copy-start | bytes 1179652
  9.1 135.6 %collective-permute-start = (bf16[64,3072]{1,0:T(8,128)(2,1)S(1)}, bf16[64,3072]{1,0:T(8,128)(2,1)}, u32[]{:S(2)}, u32[]{:S(2)}) collective-permute-start(bf16[64,3072]{1,0:T(8,128)(2,1)S(1)} %pad_maximum_fusion.5), channel_id=1, source_target_pairs={{0,4},{2,6},{4,0},{6,2},{1,5},{3,7},{5,1},{7,3},{8,12},{10,14},{12... | collective-permute-start | bytes 1179656 | tf_op jit(solution)/shard_map/ppermute | solution.py:126
  144.7 57.8 %copy-start.6 = (bf16[1536,2,2,128]{3,0,2,1:T(8,128)(2,1)}, bf16[1536,2,2,128]{3,0,2,1:T(8,128)(2,1)S(1)}, u32[]{:S(2)}) copy-start(bf16[1536,2,2,128]{3,0,2,1:T(8,128)(2,1)S(1)} %copy.49) | copy-start | bytes 4718596
  159.2 331.0 %all-gather.8.cloned.1.call-start = ((), (), s32[]{:S(2)}) async-start(), calls=%async_computation.8 | async-start | bytes 19496960 | tf_op jit(solution)/shard_map/all_gather | solution.py:27
  197.0 9.6 %copy-start = (bf16[64,1536]{1,0:T(8,128)(2,1)}, bf16[64,1536]{1,0:T(8,128)(2,1)S(1)}, u32[]{:S(2)}) copy-start(bf16[64,1536]{1,0:T(8,128)(2,1)S(1)} %get-tuple-element.37) | copy-start | bytes 589828
  197.0 354.3 %all-gather.6.cloned.1.call-start = ((), (), s32[]{:S(2)}) async-start(), calls=%async_computation.7 | async-start | bytes 6684672 | tf_op jit(solution)/shard_map/all_gather | solution.py:27
  197.0 56.7 %collective-permute-start.1 = (bf16[1536,8960]{1,0:T(8,128)(2,1)}, bf16[1536,8960]{1,0:T(8,128)(2,1)}, u32[]{:S(2)}, u32[]{:S(2)}) collective-permute-start(bf16[1536,8960]{1,0:T(8,128)(2,1)} %get-tuple-element.26), channel_id=1, source_target_pairs={{0,1},{1,0},{2,3},{3,2},{4,5},{5,4},{6,7},{7,6},{8,9},{9,8},{10,11... | collective-permute-start | bytes 82575368 | tf_op jit(solution)/shard_map/ppermute | solution.py:141
  197.1 93.9 %collective-permute-start.3 = (bf16[1536,1536]{1,0:T(8,128)(2,1)}, bf16[1536,1536]{1,0:T(8,128)(2,1)}, u32[]{:S(2)}, u32[]{:S(2)}) collective-permute-start(bf16[1536,1536]{1,0:T(8,128)(2,1)} %get-tuple-element.27), channel_id=1, source_target_pairs={{0,1},{1,0},{2,3},{3,2},{4,5},{5,4},{6,7},{7,6},{8,9},{9,8},{10,11... | collective-permute-start | bytes 14155784 | tf_op jit(solution)/shard_map/ppermute | solution.py:141
  197.7 363.9 %reduce-scatter.5.cloned.1.call-start = ((), (), s32[]{:S(2)}) async-start(), calls=%async_computation.5 | async-start | bytes 30965760 | tf_op jit(solution)/shard_map/reduce_scatter | solution.py:31
  216.2 36.3 %collective-permute-start.2 = (bf16[1536,512]{0,1:T(8,128)(2,1)S(1)}, bf16[1536,512]{0,1:T(8,128)(2,1)S(1)}, u32[]{:S(2)}, u32[]{:S(2)}) collective-permute-start(bf16[1536,512]{0,1:T(8,128)(2,1)S(1)} %pad_maximum_fusion.1), channel_id=1, source_target_pairs={{0,1},{1,0},{2,3},{3,2},{4,5},{5,4},{6,7},{7,6},{8,9},{9,8},{10,11... | collective-permute-start | bytes 4718600 | tf_op jit(solution)/shard_map/ppermute | solution.py:141
  221.1 31.4 %copy-start.17 = (bf16[1536,1536]{1,0:T(8,128)(2,1)}, bf16[1536,1536]{1,0:T(8,128)(2,1)S(1)}, u32[]{:S(2)}) copy-start(bf16[1536,1536]{1,0:T(8,128)(2,1)S(1)} %convolution_convert_fusion.2) | copy-start | bytes 14155780
  291.0 458.0 %reduce-scatter.3.cloned.1.call-start = ((), (), s32[]{:S(2)}) async-start(), calls=%async_computation.4 | async-start | bytes 32735232 | tf_op jit(solution)/shard_map/reduce_scatter | solution.py:31
  291.0 136.8 %collective-permute-start.5 = (bf16[1536,1536]{1,0:T(8,128)(2,1)}, bf16[1536,1536]{1,0:T(8,128)(2,1)}, u32[]{:S(2)}, u32[]{:S(2)}) collective-permute-start(bf16[1536,1536]{1,0:T(8,128)(2,1)} %bitcast.199), channel_id=1, source_target_pairs={{0,1},{1,0},{2,3},{3,2},{4,5},{5,4},{6,7},{7,6},{8,9},{9,8},{10,11... | collective-permute-start | bytes 14155784 | tf_op jit(solution)/shard_map/ppermute | solution.py:141
  344.4 83.5 %collective-permute-start.4 = (bf16[1536,4480]{1,0:T(8,128)(2,1)}, bf16[1536,4480]{1,0:T(8,128)(2,1)}, u32[]{:S(2)}, u32[]{:S(2)}) collective-permute-start(bf16[1536,4480]{1,0:T(8,128)(2,1)} %fusion.9), channel_id=1, source_target_pairs={{0,1},{1,0},{2,3},{3,2},{4,5},{5,4},{6,7},{7,6},{8,9},{9,8},{10,11... | collective-permute-start | bytes 41287688 | tf_op jit(solution)/shard_map/ppermute | solution.py:141
  392.5 31.6 %copy-start.15 = (bf16[1536,512]{0,1:T(8,128)(2,1)S(1)}, bf16[1536,512]{0,1:T(8,128)(2,1)}, u32[]{:S(2)}) copy-start(bf16[1536,512]{0,1:T(8,128)(2,1)} %copy-done.14) | copy-start | bytes 4718596
  392.5 31.6 %copy-start.16 = (f32[1536,256]{1,0:T(8,128)S(1)}, f32[1536,256]{1,0:T(8,128)}, u32[]{:S(2)}) copy-start(f32[1536,256]{1,0:T(8,128)} %fusion.73) | copy-start | bytes 4718596
  490.2 12.4 %copy-start.7 = (bf16[1536,2,2,128]{3,0,2,1:T(8,128)(2,1)S(1)}, bf16[1536,2,2,128]{3,0,2,1:T(8,128)(2,1)}, u32[]{:S(2)}) copy-start(bf16[1536,2,2,128]{3,0,2,1:T(8,128)(2,1)} %copy-done.6) | copy-start | bytes 4718596
  490.2 12.4 %copy-start.5 = (bf16[2,384,1536]{2,1,0:T(8,128)(2,1)S(1)}, bf16[2,384,1536]{2,1,0:T(8,128)(2,1)}, u32[]{:S(2)}) copy-start(bf16[2,384,1536]{2,1,0:T(8,128)(2,1)} %copy-done.4) | copy-start | bytes 7077892
  505.9 40.9 %all-to-all-start = ((bf16[64,16,752]{2,0,1:T(8,128)(2,1)}), bf16[64,16,752]{2,0,1:T(8,128)(2,1)S(1)}, u32[]{:S(2)}, u32[]{:S(2)}) async-start(bf16[64,16,752]{2,0,1:T(8,128)(2,1)} %pad_maximum_fusion.2), calls=%async_computation.2 | async-start | bytes 3145728 | tf_op jit(solution)/shard_map/all_to_all | solution.py:209
  513.1 270.3 %collective-permute-start.6 = (bf16[64,1536]{1,0:T(8,128)(2,1)}, bf16[64,1536]{1,0:T(8,128)(2,1)S(1)}, u32[]{:S(2)}, u32[]{:S(2)}) collective-permute-start(bf16[64,1536]{1,0:T(8,128)(2,1)} %fusion.56), channel_id=1, source_target_pairs={{0,4},{2,6},{4,0},{6,2},{1,5},{3,7},{5,1},{7,3},{8,12},{10,14},{12... | collective-permute-start | bytes 589832 | tf_op jit(solution)/shard_map/ppermute | solution.py:206
  558.6 230.8 %all-to-all-start.1 = ((f32[16,96,192]{1,2,0:T(8,128)}), f32[16,96,192]{1,2,0:T(8,128)S(1)}, u32[]{:S(2)}, u32[]{:S(2)}) async-start(f32[16,96,192]{1,2,0:T(8,128)} %copy.61), calls=%async_computation.3 | async-start | bytes 3145728 | tf_op jit(solution)/shard_map/all_to_all | solution.py:219
  565.0 230.1 %collective-permute-start.8 = (f32[560,768]{1,0:T(8,128)}, f32[560,768]{1,0:T(8,128)}, u32[]{:S(2)}, u32[]{:S(2)}) collective-permute-start(f32[560,768]{1,0:T(8,128)} %get-tuple-element.53), channel_id=1, source_target_pairs={{0,1},{1,0},{2,3},{3,2},{4,5},{5,4},{6,7},{7,6},{8,9},{9,8},{10,11... | collective-permute-start | bytes 5160968 | tf_op jit(solution)/shard_map/ppermute | solution.py:141
  751.8 47.9 %collective-permute-start.7 = (f32[96,4736]{1,0:T(8,128)}, f32[96,4736]{1,0:T(8,128)}, u32[]{:S(2)}, u32[]{:S(2)}) collective-permute-start(f32[96,4736]{1,0:T(8,128)} %constant_dynamic-slice_fusion), channel_id=1, source_target_pairs={{0,1},{1,0},{2,3},{3,2},{4,5},{5,4},{6,7},{7,6},{8,9},{9,8},{10,11... | collective-permute-start | bytes 5455880 | tf_op jit(solution)/shard_map/ppermute | solution.py:141
  (10 other events, 36.0 us)
Sparse Core Ops, SparseCore 0:
  159.3 42.7 all-gather.3
  204.4 81.5 all-gather.7
  288.8 61.2 all-gather.5
Sparse Core Ops, SparseCore 1:
  291.1 215.0 reduce-scatter.4
  510.3 238.6 reduce-scatter.2

commit v5 on v3

--- a/solution.py
+++ b/solution.py
@@ -124,9 +124,8 @@
         prob_bf = prob.astype(BF16)
         ctx = flat_of(bdot(prob_bf, val_h, 2, 1).astype(BF16))
         mid = (hid.astype(F32) + dot(ctx, w_o, 1, 0)).astype(BF16)
-        cm_all = gather(jnp.concatenate([ctx, mid], axis=1))
-        ctx_all, mid_all = cm_all[:, :d_model], cm_all[:, d_model:]
-        dec_act, dec_gpre, g_mid = dec_mlp(mid, cot, w_1, w_2, w_1.shape[1] // 10)
+        ctx_all = gather(ctx)
+        dec_act, dec_gpre, g_mid = dec_mlp(mid, cot, w_1, w_2, w_1.shape[1] // 7)
         gpre_all = gather(dec_gpre)
         g_ctx = heads_of(dot(g_mid, w_o, 1, 1).astype(BF16))
         g_prob = bdot(g_ctx, val_h, 2, 2)
@@ -168,15 +167,14 @@
         dh = (g_mid.astype(F32) + dot(g_query, w_q, 1, 1)).astype(BF16)
         dh = lax.ppermute(dh, 'chip', partner_perm)
 
-        sent = [t.reshape(s_dec, n_dev, -1) for t in (dec_act, g_mid, g_query)]
+        sent = [t.reshape(s_dec, n_dev, -1) for t in (dec_act, g_mid, g_query, mid)]
         cols = lax.all_to_all(jnp.concatenate(sent, axis=2), AXES, split_axis=1, concat_axis=0, tiled=True)
         cols = cols.reshape(n_dev * s_dec, -1)
-        gmid_c = cols[:, n2:n2 + n1]
+        gmid_c, mid_c = cols[:, n2:n2 + n1], cols[:, n2 + 2 * n1:]
         halves = cols.reshape(n_data, 2, chips // 2, 2 * s_dec, -1)
         cols = jnp.concatenate([halves[:, 1:], halves[:, :1]], axis=1).reshape(n_dev * s_dec, -1)
-        act_c, gq_c = cols[:, :n2], cols[:, n2 + n1:]
+        act_c, gq_c = cols[:, :n2], cols[:, n2 + n1:n2 + 2 * n1]
         g_w2 = dot(act_c, cot_all, 0, 0)
-        mid_c = lax.dynamic_slice_in_dim(mid_all, lax.axis_index(AXES) * n1, n1, 1)
         g_w1 = dot(mid_c, gpre_all, 0, 0)
         blocks = jnp.concatenate([dot(ctx_all, gmid_c, 0, 0), dot(hid_all, gq_c, 0, 0)], axis=1)
         blocks = lax.all_to_all(blocks.reshape(n_dev, n1, -1), AXES, split_axis=0, concat_axis=0, tiled=True)

time: 814 us -> 832 us (1.022)
  waiting for transfers between devices: 184 us -> 207 us
    reduce_scatter x2, waiting for transfers between devices: 183 us -> 206 us  [scatter(): return lax.psum_scatter(own, CHIPS, scatter_dimension=0, tiled=True)]
  transfers between devices with their start and end apart: 16 -> 16, of which waited for: 1 -> 1; matrix products, arithmetic and copies ran while one was open for 66% -> 58% of each run, Pallas kernels for 5% -> 4%
where the time goes in v5:
time: 832 us; the launch traced here: 826 us
  matrix products  485 us (58%)
  waiting for transfers between devices  207 us (25%)
  Pallas kernels  37.1 us (4%)
  local copies, waits for them, and re-layouts  35.3 us (4%)
  other arithmetic  30.9 us (4%)
  between operations  16.2 us (2%)
  starting transfers between devices  13.8 us (2%)
    dot_general x22, matrix products, dot(): lax.dot_general(lhs, rhs, (((lhs_dim,), (rhs_dim,)), ((), ())), preferred...  466 us
    reduce_scatter x2, waiting for transfers between devices, scatter(): return lax.psum_scatter(own, CHIPS, scatter_dimension=0, tiled=True)  206 us
    pallas_call x1, Pallas kernels, dec_mlp(): pl.pallas_call(dec_mlp_kernel, grid=(width // block,), in_specs=[rows, ro...  37.1 us
    concatenate x1, other arithmetic, step(): jnp.concatenate([up_half, wkv_half], axis=1)  20.7 us
  transfers between devices with their start and end apart: 16, of which 1 were waited for; matrix products, arithmetic and copies ran while one was open for 58% of the time, Pallas kernels for 4%

profile of v5, /device:TPU:0, one launch (start us, length us, event | category | flops | bytes accessed | tf_op | source)
XLA Modules:
  0.0 826.1 jit_solution(10931167408248932480)
XLA Ops:
  8.1 61.5 %fusion.9 = (bf16[1536,8960]{1,0:T(8,128)(2,1)}, f32[1536,8960]{1,0:T(8,128)}) fusion(bf16[1,1536,8960]{2,1,0:T(8,128)(2,1)} %param.14, bf16[1,1536,1536]{2,1,0:T(8,128)(2,1)} %param.11), kind=kOutput, calls=%fused_computation.10 | convolution fusion | flops 42402447360 | bytes 114819072 | tf_op jit(solution)/shard_map/dot_general | solution.py:17
  74.9 55.8 %add_convert_fusion.1 = bf16[1536,1536]{1,0:T(8,128)(2,1)} fusion(bf16[1536,8960]{1,0:T(8,128)(2,1)} %get-tuple-element.58, bf16[1,8960,1536]{2,1,0:T(8,128)(2,1)} %param.15, bf16[1,1536,1536]{2,1,0:T(8,128)(2,1)} %param.11), kind=kOutput, calls=%fused_computation.61 | convolution fusion | flops 42285662208 | bytes 64487424 | tf_op jit(solution)/shard_map/dot_general | solution.py:17
  130.7 6.6 convolution_convert_fusion.4
  154.9 37.1 %shard_map.186 = (bf16[64,8960]{1,0:T(8,128)(2,1)S(1)}, bf16[64,8960]{1,0:T(8,128)(2,1)}, bf16[64,1536]{1,0:T(8,128)(2,1)S(1)}) custom-call(bf16[64,1536]{1,0:T(8,128)(2,1)S(1)} %add_convert_fusion.2.mid_ref, bf16[64,1536]{1,0:T(8,128)(2,1)S(1)} %slice.99.cot_ref, bf16[1536,8960]{1,0:T(8,128)(2,1)} %bitcast.179, bf16[8960,1536]{1,0:T(8,128)(2,1)} %bitcast.180), custom_call_target="tpu_custom_call" | custom-call | flops 5284823040 | bytes 55050240 | tf_op jit(solution)/shard_map/pallas_call | solution.py:54
  197.6 6.1 multiply_convert_fusion
  207.1 4.6 convolution_convert_fusion.2
  211.8 30.7 %fusion.62 = f32[8960,768]{1,0:T(8,128)} fusion(bf16[1536,8960]{1,0:T(8,128)(2,1)} %get-tuple-element.58, bf16[1536,1536]{1,0:T(8,128)(2,1)S(1)} %convolution_convert_fusion.2, u32[]{:T(128)S(6)} %mul.148), kind=kOutput, calls=%fused_computation.89 | convolution fusion | flops 21139292160 | bytes 57409540 | tf_op jit(solution)/shard_map/dot_general | solution.py:17
  243.6 37.3 %convolution_add_fusion = f32[8960,768]{1,0:T(8,128)} fusion(f32[8960,768]{1,0:T(8,128)} %fusion.62, bf16[1536,8960]{1,0:T(8,128)(2,1)} %collective-permute-done.1, bf16[1536,512]{0,1:T(8,128)(2,1)} %copy-done.20, bf16[1536,512]{1,0:T(8,128)(2,1)} %bitcast_dynamic-update-slice_fusion, u32[]{:T(128)S(6)} %mul.148), kind=kOutput, calls=%fused_computation.48 | convolution fusion | flops 22355312640 | bytes 84934656 | tf_op jit(solution)/shard_map/dot_general | solution.py:17
  282.4 4.9 fusion.85
  287.3 46.8 %fusion.17 = bf16[1536,4480]{1,0:T(8,128)(2,1)} fusion(f32[1536,8960]{1,0:T(8,128)} %get-tuple-element.59, u32[]{:T(128)S(6)} %mul.163, bf16[1536,1536]{1,0:T(8,128)(2,1)} %copy-done.23, bf16[1,8960,1536]{2,1,0:T(8,128)(2,1)} %param.15), kind=kOutput, calls=%fused_computation.27 | convolution fusion | flops 21290680320 | bytes 59769856 | tf_op jit(solution)/shard_map/dot_general | solution.py:17
  334.8 47.7 %fusion.12 = bf16[1536,4480]{1,0:T(8,128)(2,1)} fusion(f32[1536,8960]{1,0:T(8,128)} %get-tuple-element.59, u32[]{:T(128)S(6)} %mul.149, bf16[1536,1536]{1,0:T(8,128)(2,1)} %copy-done.23, bf16[1,8960,1536]{2,1,0:T(8,128)(2,1)} %param.15), kind=kOutput, calls=%fused_computation.22 | convolution fusion | flops 21290680320 | bytes 59769856 | tf_op jit(solution)/shard_map/dot_general | solution.py:17
  382.5 30.6 %convolution_bitcast_fusion = f32[1536,4480]{1,0:T(8,128)} fusion(bf16[1536,4480]{1,0:T(8,128)(2,1)} %fusion.12, bf16[1,1536,1536]{2,1,0:T(8,128)(2,1)} %param.11), kind=kOutput, calls=%fused_computation.45 | convolution fusion | flops 21139292160 | bytes 46006272 | tf_op jit(solution)/shard_map/dot_general | solution.py:17
  413.2 4.2 convolution_add_fusion.1
  417.4 35.4 %bitcast_add_fusion = f32[1536,4480]{1,0:T(8,128)} fusion(f32[1536,4480]{1,0:T(8,128)} %convolution_bitcast_fusion, bf16[1536,4480]{1,0:T(8,128)(2,1)} %collective-permute-done.4, bf16[1536,1536]{1,0:T(8,128)(2,1)} %collective-permute-done.5), kind=kOutput, calls=%fused_computation.40 | convolution fusion | flops 21146173440 | bytes 73531392 | tf_op jit(solution)/shard_map/dot_general | solution.py:17
  452.8 20.7 %pad_maximum_fusion = f32[1536,4736]{1,0:T(8,128)} fusion(f32[1536,256]{1,0:T(8,128)S(1)} %convolution_add_fusion.1, f32[1536,4480]{1,0:T(8,128)} %bitcast_add_fusion), kind=kLoop, calls=%fused_computation.19 | loop fusion | flops 7274496 | bytes 58195968 | tf_op jit(solution)/shard_map/concatenate | solution.py:155
  487.2 4.0 fusion.68
  493.2 30.9 %fusion.36 = f32[1536,1536]{1,0:T(8,128)} fusion(bf16[1536,4480]{1,0:T(8,128)(2,1)} %fusion.12, bf16[1,1536,8960]{2,1,0:T(8,128)(2,1)} %param.14, u32[]{:T(128)S(6)} %mul.149), kind=kOutput, calls=%fused_computation.51 | convolution fusion | flops 21139292160 | bytes 36962308 | tf_op jit(solution)/shard_map/dot_general | solution.py:17
  524.1 32.1 %fusion.46 = bf16[1,1536,1536]{2,1,0:T(8,128)(2,1)} fusion(f32[1536,1536]{1,0:T(8,128)} %fusion.36, bf16[1536,1536]{1,0:T(8,128)(2,1)} %copy-done.23, bf16[1536,4480]{1,0:T(8,128)(2,1)} %fusion.17, bf16[1,1536,8960]{2,1,0:T(8,128)(2,1)} %param.14, u32[]{:T(128)S(6)} %mul.163), kind=kOutput, calls=%fused_computation.63 | convolution fusion | flops 21148729344 | bytes 46399492 | tf_op jit(solution)/shard_map/dot_general | solution.py:17
  557.9 3.9 fusion.96
  573.0 4.1 dynamic-slice_bitcast_fusion.1
  577.4 206.2 %reduce-scatter.3.cloned.1.call-done = f32[192,4736]{1,0:T(8,128)} async-done(((f32[1536,4736]{1,0:T(8,128)}), f32[192,4736]{1,0:T(8,128)}) %reduce-scatter.3.cloned.1.call-update) | async-done | bytes 3637264 | tf_op jit(solution)/shard_map/reduce_scatter | solution.py:29
  786.4 11.3 %convolution_bitcast_fusion.1 = f32[1,96,8960]{2,1,0:T(8,128)} fusion(bf16[1024,8960]{1,0:T(8,128)(2,1)} %all-gather.8.cloned.1.call-done, bf16[1024,848]{1,0:T(8,128)(2,1)S(1)} %bitcast.185), kind=kOutput, calls=%fused_computation.59 | convolution fusion | flops 1761607680 | bytes 22052864 | tf_op jit(solution)/shard_map/dot_general | solution.py:17
  797.8 5.6 convolution_bitcast_fusion.2
  807.2 4.4 maximum_select_fusion.1
  (141 shorter events, 77.2 us)
Async XLA Ops:
  8.0 62.3 %copy-start.19 = (bf16[1,64,1536]{2,1,0:T(8,128)(2,1)S(1)}, bf16[1,64,1536]{2,1,0:T(8,128)(2,1)}, u32[]{:S(2)}) copy-start(bf16[1,64,1536]{2,1,0:T(8,128)(2,1)} %param.12) | copy-start | bytes 589828
  8.0 62.3 %copy-start.18 = (bf16[1,64,1536]{2,1,0:T(8,128)(2,1)S(1)}, bf16[1,64,1536]{2,1,0:T(8,128)(2,1)}, u32[]{:S(2)}) copy-start(bf16[1,64,1536]{2,1,0:T(8,128)(2,1)} %param.13) | copy-start | bytes 589828
  8.0 64.9 %copy-start.15 = (bf16[1,1536,2,128]{3,2,1,0:T(2,128)(2,1)S(1)}, bf16[1,1536,2,128]{3,2,1,0:T(2,128)(2,1)}, u32[]{:S(2)}) copy-start(bf16[1,1536,2,128]{3,2,1,0:T(2,128)(2,1)} %param.16) | copy-start | bytes 2359300
  8.0 65.8 %copy-start.16 = (bf16[1,1536,2,128]{3,2,1,0:T(2,128)(2,1)S(1)}, bf16[1,1536,2,128]{3,2,1,0:T(2,128)(2,1)}, u32[]{:S(2)}) copy-start(bf16[1,1536,2,128]{3,2,1,0:T(2,128)(2,1)} %param.17) | copy-start | bytes 2359300
  8.1 549.8 %all-gather.4.cloned.1.call-start = ((), (), s32[]{:S(2)}) async-start(), calls=%async_computation.6 | async-start | bytes 3342336 | tf_op jit(solution)/shard_map/all_gather | solution.py:25
  69.6 174.1 %collective-permute-start.1 = (bf16[1536,8960]{1,0:T(8,128)(2,1)}, bf16[1536,8960]{1,0:T(8,128)(2,1)}, u32[]{:S(2)}, u32[]{:S(2)}) collective-permute-start(bf16[1536,8960]{1,0:T(8,128)(2,1)} %get-tuple-element.58), channel_id=1, source_target_pairs={{0,1},{1,0},{2,3},{3,2},{4,5},{5,4},{6,7},{7,6},{8,9},{9,8},{10,11... | collective-permute-start | bytes 82575368 | tf_op jit(solution)/shard_map/ppermute | solution.py:102
  70.3 60.4 %copy-start.13 = (bf16[64,3072]{1,0:T(8,128)(2,1)}, bf16[64,3072]{1,0:T(8,128)(2,1)S(1)}, u32[]{:S(2)}) copy-start(bf16[64,3072]{1,0:T(8,128)(2,1)S(1)} %pad_maximum_fusion.5) | copy-start | bytes 1179652
  70.3 69.1 %collective-permute-start = (bf16[64,3072]{1,0:T(8,128)(2,1)S(1)}, bf16[64,3072]{1,0:T(8,128)(2,1)S(1)}, u32[]{:S(2)}, u32[]{:S(2)}) collective-permute-start(bf16[64,3072]{1,0:T(8,128)(2,1)S(1)} %pad_maximum_fusion.5), channel_id=1, source_target_pairs={{0,4},{2,6},{4,0},{6,2},{1,5},{3,7},{5,1},{7,3},{8,12},{10,14},{12... | collective-permute-start | bytes 1179656 | tf_op jit(solution)/shard_map/ppermute | solution.py:87
  139.4 55.1 %copy-start.10 = (bf16[1536,2,2,128]{3,0,2,1:T(8,128)(2,1)}, bf16[1536,2,2,128]{3,0,2,1:T(8,128)(2,1)S(1)}, u32[]{:S(2)}) copy-start(bf16[1536,2,2,128]{3,0,2,1:T(8,128)(2,1)S(1)} %copy.49) | copy-start | bytes 4718596
  143.6 51.0 %copy-start.14 = (bf16[2,6,64,128]{3,2,1,0:T(8,128)(2,1)}, bf16[2,6,64,128]{3,2,1,0:T(8,128)(2,1)S(1)}, u32[]{:S(2)}) copy-start(bf16[2,6,64,128]{3,2,1,0:T(8,128)(2,1)S(1)} %copy.48) | copy-start | bytes 589828
  150.5 411.3 %all-gather.6.cloned.1.call-start = ((), (), s32[]{:S(2)}) async-start(), calls=%async_computation.7 | async-start | bytes 6684672 | tf_op jit(solution)/shard_map/all_gather | solution.py:25
  150.5 130.4 %collective-permute-start.3 = (bf16[1536,1536]{1,0:T(8,128)(2,1)}, bf16[1536,1536]{1,0:T(8,128)(2,1)}, u32[]{:S(2)}, u32[]{:S(2)}) collective-permute-start(bf16[1536,1536]{1,0:T(8,128)(2,1)} %add_convert_fusion.1), channel_id=1, source_target_pairs={{0,1},{1,0},{2,3},{3,2},{4,5},{5,4},{6,7},{7,6},{8,9},{9,8},{10,11... | collective-permute-start | bytes 14155784 | tf_op jit(solution)/shard_map/ppermute | solution.py:102
  151.3 421.8 %reduce-scatter.5.cloned.1.call-start = ((), (), s32[]{:S(2)}) async-start(), calls=%async_computation.5 | async-start | bytes 30965760 | tf_op jit(solution)/shard_map/reduce_scatter | solution.py:29
  151.3 41.3 %slice-start = ((s8[4718592]{0:T(1024)(128)(4,1)}), s8[4194304]{0:T(1024)(128)(4,1)S(1)}, s32[]{:S(2)}) async-start(s8[4718592]{0:T(1024)(128)(4,1)} %bitcast.181), calls=%async_computation.9 | async-start | bytes 8388608
  206.9 35.6 %collective-permute-start.2 = (bf16[1536,512]{0,1:T(8,128)(2,1)S(1)}, bf16[1536,512]{0,1:T(8,128)(2,1)S(1)}, u32[]{:S(2)}, u32[]{:S(2)}) collective-permute-start(bf16[1536,512]{0,1:T(8,128)(2,1)S(1)} %pad_maximum_fusion.3), channel_id=1, source_target_pairs={{0,1},{1,0},{2,3},{3,2},{4,5},{5,4},{6,7},{7,6},{8,9},{9,8},{10,11... | collective-permute-start | bytes 4718600 | tf_op jit(solution)/shard_map/ppermute | solution.py:102
  281.0 502.6 %reduce-scatter.3.cloned.1.call-start = ((), (), s32[]{:S(2)}) async-start(), calls=%async_computation.4 | async-start | bytes 32735232 | tf_op jit(solution)/shard_map/reduce_scatter | solution.py:29
  281.1 136.3 %collective-permute-start.5 = (bf16[1536,1536]{1,0:T(8,128)(2,1)}, bf16[1536,1536]{1,0:T(8,128)(2,1)}, u32[]{:S(2)}, u32[]{:S(2)}) collective-permute-start(bf16[1536,1536]{1,0:T(8,128)(2,1)} %bitcast.214), channel_id=1, source_target_pairs={{0,1},{1,0},{2,3},{3,2},{4,5},{5,4},{6,7},{7,6},{8,9},{9,8},{10,11... | collective-permute-start | bytes 14155784 | tf_op jit(solution)/shard_map/ppermute | solution.py:102
  334.1 83.3 %collective-permute-start.4 = (bf16[1536,4480]{1,0:T(8,128)(2,1)}, bf16[1536,4480]{1,0:T(8,128)(2,1)}, u32[]{:S(2)}, u32[]{:S(2)}) collective-permute-start(bf16[1536,4480]{1,0:T(8,128)(2,1)} %fusion.17), channel_id=1, source_target_pairs={{0,1},{1,0},{2,3},{3,2},{4,5},{5,4},{6,7},{7,6},{8,9},{9,8},{10,11... | collective-permute-start | bytes 41287688 | tf_op jit(solution)/shard_map/ppermute | solution.py:102
  473.5 312.9 %all-gather.8.cloned.1.call-start = ((), (), s32[]{:S(2)}) async-start(), calls=%async_computation.8 | async-start | bytes 19496960 | tf_op jit(solution)/shard_map/all_gather | solution.py:25
  483.6 72.6 %all-to-all-start = ((bf16[64,16,848]{2,0,1:T(8,128)(2,1)}), bf16[64,16,848]{2,0,1:T(8,128)(2,1)S(1)}, u32[]{:S(2)}, u32[]{:S(2)}) async-start(bf16[64,16,848]{2,0,1:T(8,128)(2,1)} %pad_maximum_fusion.1), calls=%async_computation.2 | async-start | bytes 3670016 | tf_op jit(solution)/shard_map/all_to_all | solution.py:171
  491.2 65.0 %collective-permute-start.6 = (bf16[64,1536]{1,0:T(8,128)(2,1)S(1)}, bf16[64,1536]{1,0:T(8,128)(2,1)S(1)}, u32[]{:S(2)}, u32[]{:S(2)}) collective-permute-start(bf16[64,1536]{1,0:T(8,128)(2,1)S(1)} %fusion.68), channel_id=1, source_target_pairs={{0,4},{2,6},{4,0},{6,2},{1,5},{3,7},{5,1},{7,3},{8,12},{10,14},{12... | collective-permute-start | bytes 589832 | tf_op jit(solution)/shard_map/ppermute | solution.py:168
  569.8 233.6 %all-to-all-start.1 = ((f32[16,96,192]{1,2,0:T(8,128)}), f32[16,96,192]{1,2,0:T(8,128)}, u32[]{:S(2)}, u32[]{:S(2)}) async-start(f32[16,96,192]{1,2,0:T(8,128)} %copy.62), calls=%async_computation.3 | async-start | bytes 3145728 | tf_op jit(solution)/shard_map/all_to_all | solution.py:180
  577.1 230.1 %collective-permute-start.8 = (f32[560,768]{1,0:T(8,128)}, f32[560,768]{1,0:T(8,128)}, u32[]{:S(2)}, u32[]{:S(2)}) collective-permute-start(f32[560,768]{1,0:T(8,128)} %get-tuple-element.47), channel_id=1, source_target_pairs={{0,1},{1,0},{2,3},{3,2},{4,5},{5,4},{6,7},{7,6},{8,9},{9,8},{10,11... | collective-permute-start | bytes 5160968 | tf_op jit(solution)/shard_map/ppermute | solution.py:102
  786.4 25.4 %collective-permute-start.7 = (f32[96,4736]{1,0:T(8,128)}, f32[96,4736]{1,0:T(8,128)}, u32[]{:S(2)}, u32[]{:S(2)}) collective-permute-start(f32[96,4736]{1,0:T(8,128)} %constant_dynamic-slice_fusion), channel_id=1, source_target_pairs={{0,1},{1,0},{2,3},{3,2},{4,5},{5,4},{6,7},{7,6},{8,9},{9,8},{10,11... | collective-permute-start | bytes 5455880 | tf_op jit(solution)/shard_map/ppermute | solution.py:102
  (18 other events, 213.4 us)
Sparse Core Ops, SparseCore 0:
  150.6 32.0 all-gather.3
  185.5 42.1 all-gather.5
  476.6 139.6 all-gather.7
Sparse Core Ops, SparseCore 1:
  281.1 196.1 reduce-scatter.4
  481.4 302.1 reduce-scatter.2
